TPU v7x, 32 devices: a whole 2x2x4 slice. The times are simulated.
32 devices in a mesh: row: 4 (over y, core), col: 8 (over z, x).
Axes of the slice: x: 2, y: 2, z: 4, core: 2. Of those that a mesh axis runs over, the one named last changes fastest.
Arguments:
- density: float32 [4096, 32768], P('row', 'col'), may hold values from 0 to 1
- design_mask: int32 [32, 256], P('row', 'col'), may hold values 0 or 1
- rebalance: int32 [8192], replicated, may hold values from 0 to 8191, as said below
Outputs:
- balanced: bfloat16 [8192, 128, 128], P(('row', 'col'))
- constraint: float32 [], replicated
Inputs may be any that keep to these rules, and one draw needn't show every extreme that they name: `rebalance`: A permutation of the 8192 block numbers. Of the blocks that one device holds, the ones that land among one device's output blocks number exactly 8 or none.
All inputs are finite; a program needn't handle non-finite values. No bound on the sum of `design_mask` on one device may be relied on, other than what follows from the above.
Results may differ from a plain program's by a relative error of at most 0.001.
Values may be sent and summed in bfloat16 or wider, within the bound.
No kernel may reach another device: no remote copies, remote signals or barrier semaphores. Data moves between devices by JAX's collectives and lax.ppermute only.
A program may use at most 192 MiB of HBM per device.

v0:
```python
import functools

import jax
import jax.numpy as jnp
import numpy as np
from jax import lax
from jax.experimental import pallas as pl
from jax.experimental.pallas import tpu as pltpu
from jax.sharding import PartitionSpec as P


BS = 128
RADIUS = 16
PAD = BS + 2 * RADIUS
WIDE = 3 * BS
BUFFERS = 4
GROUPS = (2, 4, 8, 8, 10)

SHARPNESS = 32.0
THRESHOLD = 0.5
VOLUME_TARGET = 0.4

AXES = ("row", "col")


def tap_parts():
    sigma = RADIUS / 4.0
    offsets = np.arange(2 * RADIUS + 1, dtype=np.float64) - RADIUS
    raw_taps = np.exp(-offsets * offsets / (2.0 * sigma * sigma))
    taps = raw_taps / raw_taps.sum()
    high = taps.astype(jnp.bfloat16)
    rest = taps - high.astype(np.float64)
    missing = (rest - rest.astype(jnp.bfloat16).astype(np.float64)).sum()
    rest[0] += missing / 2
    rest[-1] += missing / 2
    return high, rest.astype(jnp.bfloat16)


def band_matrices():
    parts = tap_parts()

    def bands(lag, used):
        used = used & (np.abs(lag) <= RADIUS)
        index = np.clip(lag + RADIUS, 0, 2 * RADIUS)
        return [np.where(used, part[index], np.zeros((), part.dtype)) for part in parts]

    lane = np.arange(2 * BS)[:, None]
    source = np.where(lane < 2 * BS - RADIUS, lane, lane - 2 * BS)
    used = (lane < BS + RADIUS) | (lane >= 2 * BS - RADIUS)
    columns = bands(source - np.arange(BS)[None, :], used)
    lag = np.arange(PAD)[None, :] - RADIUS - np.arange(BS)[:, None]
    rows = bands(lag, np.ones_like(lag, bool))
    return (jnp.asarray(np.concatenate(columns, axis=1)),
            jnp.asarray(np.concatenate([rows[0], rows[0], rows[1]], axis=1)))


def exchange_order(row_count, col_count):
    device_count = row_count * col_count
    quarter = max(1, col_count // 4)
    long_part = [2, 3, 1] if col_count >= 4 else [1]
    rest = [r * col_count + c for r in range(row_count) for c in range(quarter)]
    far = [long * quarter + other for other in rest for long in long_part]
    near = [other for other in rest if other]
    order = []
    while far or near:
        order, far = order + far[:3], far[3:]
        if near:
            order.append(near.pop(0))
    order = [d for d in order if 0 < d < device_count]
    assert sorted(order) == list(range(1, device_count))
    return order


def with_halo(density):
    rows, cols = density.shape

    def moves(axis):
        up = [(i, i + 1) for i in range(lax.axis_size(axis) - 1)]
        return up, [(j, i) for i, j in up]

    up, down = moves("row")
    top = lax.ppermute(density[rows - RADIUS:], "row", up)
    bottom = lax.ppermute(density[:RADIUS], "row", down)
    up, down = moves("col")

    def strip(start):
        parts = [a[:, start:start + RADIUS].T for a in (top, density, bottom)]
        return jnp.concatenate(parts, axis=1)

    left = lax.ppermute(strip(cols - RADIUS), "col", up)
    right = lax.ppermute(strip(0), "col", down)
    left = jnp.pad(left, ((BS - RADIUS, 0), (0, 0))).T
    right = jnp.pad(right, ((0, BS - RADIUS), (0, 0))).T
    return top, bottom, left, right


def block_tables(rebalance, me, mask_rows, mask_cols, row_count, col_count, capacity, order):
    device_count = row_count * col_count
    block_count = mask_rows * mask_cols
    wanted = rebalance.reshape(device_count, block_count)
    block_row = lax.div(wanted, mask_cols * col_count)
    block_col = lax.rem(wanted, mask_cols * col_count)
    source = lax.div(block_row, mask_rows) * col_count + lax.div(block_col, mask_cols)
    local = lax.rem(block_row, mask_rows) * mask_cols + lax.rem(block_col, mask_cols)
    slots = jnp.arange(block_count, dtype=jnp.int32)
    devices = jnp.arange(device_count, dtype=jnp.int32)
    mine = lax.dynamic_index_in_dim(source, me, 0, keepdims=True)
    match = jnp.concatenate([source == me, mine == devices[:, None]], axis=0)
    value = jnp.concatenate([local, jnp.broadcast_to(slots, local.shape)], axis=0)
    before = (slots[:, None] < slots[None, :]).astype(jnp.bfloat16)
    rank = jnp.dot(match.astype(jnp.bfloat16), before, preferred_element_type=jnp.float32)
    rank = jnp.where(match, rank.astype(jnp.int32), -1)
    ranks = jnp.arange(capacity, dtype=jnp.int32)
    chosen = rank[:, None, :] == ranks[None, :, None]
    table = jnp.sum(jnp.where(chosen, value[:, None, :], 0), axis=2)
    partner = me ^ jnp.array(order, jnp.int32)
    pick = partner[:, None] == devices[None, :]
    table = table.reshape(2, 1, device_count, capacity)
    return jnp.sum(jnp.where(pick[None, :, :, None], table, 0), axis=2).reshape(-1)


class Meta:
    def __init__(self, device_count, capacity):
        self.capacity = capacity
        self.send = 0
        self.place = device_count * capacity
        self.mask = 2 * device_count * capacity


def split_scalar(index, size):
    if size & (size - 1):
        return lax.div(index, size), lax.rem(index, size)
    return lax.shift_right_logical(index, size.bit_length() - 1), index & (size - 1)


def project_kernel(meta_ref, dens, top, bottom, left, right, wcol, wrow, acc_in, *refs,
                   layout, first, count, block_rows, block_cols, has_local):
    capacity = layout.capacity
    outs, acc_out = refs[:count], refs[count]
    buf, fetch_sem, lines, tiles, store_sem = refs[count + 1:]
    pairs = count * capacity // 2
    begin = layout.send + first * capacity

    def fetch(pair, slot):
        for half in range(2):
            block = meta_ref[begin + 2 * pair + half]
            br, bc = split_scalar(block, block_cols)
            row0 = pl.multiple_of(br * BS, BS)
            col0 = pl.multiple_of(bc * BS, BS)
            window = buf.at[slot, half]
            sem = fetch_sem.at[slot, half]
            inside = ((br > 0) & (br < block_rows - 1)) & ((bc > 0) & (bc < block_cols - 1))

            def copy(src, rows, cols):
                pltpu.make_async_copy(src, window.at[pl.ds(*rows), pl.ds(*cols)], sem).start()

            def rows_of(span, c_dst, c_len):
                @pl.when(br == 0)
                def _():
                    copy(top.at[:, span], (0, RADIUS), (c_dst, c_len))
                    copy(dens.at[pl.ds(0, PAD - RADIUS), span],
                         (RADIUS, PAD - RADIUS), (c_dst, c_len))

                @pl.when((br > 0) & (br < block_rows - 1))
                def _():
                    row1 = pl.multiple_of(row0 - RADIUS, RADIUS)
                    copy(dens.at[pl.ds(row1, PAD), span], (0, PAD), (c_dst, c_len))

                @pl.when(br == block_rows - 1)
                def _():
                    last = block_rows * BS - (PAD - RADIUS)
                    copy(dens.at[pl.ds(last, PAD - RADIUS), span],
                         (0, PAD - RADIUS), (c_dst, c_len))
                    copy(bottom.at[:, span], (PAD - RADIUS, RADIUS), (c_dst, c_len))

            @pl.when(inside)
            def _():
                row1 = pl.multiple_of(row0 - RADIUS, RADIUS)
                col1 = pl.multiple_of(col0 - BS, BS)
                pltpu.make_async_copy(
                    dens.at[pl.ds(row1, PAD), pl.ds(col1, WIDE)], window, sem).start()

            @pl.when(jnp.logical_not(inside))
            def _():
                @pl.when(bc == 0)
                def _():
                    copy(left.at[pl.ds(row0, PAD), :], (0, PAD), (0, BS))
                    rows_of(pl.ds(0, 2 * BS), BS, 2 * BS)

                @pl.when((bc > 0) & (bc < block_cols - 1))
                def _():
                    rows_of(pl.ds(pl.multiple_of(col0 - BS, BS), WIDE), 0, WIDE)

                @pl.when(bc == block_cols - 1)
                def _():
                    copy(right.at[pl.ds(row0, PAD), :], (0, PAD), (2 * BS, BS))
                    rows_of(pl.ds((block_cols - 2) * BS, 2 * BS), 0, 2 * BS)

    lower = float(np.tanh(SHARPNESS * THRESHOLD))
    upper = float(np.tanh(SHARPNESS * (1.0 - THRESHOLD)))

    def along_columns(pair):
        slot = lax.rem(pair, BUFFERS)
        lane = lax.broadcasted_iota(jnp.int32, (PAD, BS), 1)
        taps = wcol[...]
        for half in range(2):
            window = buf.at[slot, half]
            sides = jnp.where(lane < BS // 2, window[:, 2 * BS:], window[:, :BS])
            x = jnp.concatenate([window[:, BS:2 * BS], sides], axis=1)
            x_high = x.astype(jnp.bfloat16)
            x_low = (x - x_high.astype(jnp.float32)).astype(jnp.bfloat16)
            both = jnp.dot(x_high, taps, preferred_element_type=jnp.float32)
            y = both[:, :BS] + (both[:, BS:] + jnp.dot(
                x_low, taps[:, :BS], preferred_element_type=jnp.float32))
            y_high = y.astype(jnp.bfloat16)
            lanes = slice(half * BS, (half + 1) * BS)
            lines[0, :, lanes] = y_high
            lines[1, :, lanes] = (y - y_high.astype(jnp.float32)).astype(jnp.bfloat16)

    def along_rows(pair, acc):
        y_high, y_low = lines[0], lines[1]
        stacked = jnp.concatenate([y_high, y_low, y_high], axis=0)
        filtered = jnp.dot(wrow[...], stacked, preferred_element_type=jnp.float32)
        raised = lower + jnp.tanh(SHARPNESS * (filtered - THRESHOLD))
        for half in range(2):
            step = 2 * pair + half
            keep = meta_ref[layout.mask + meta_ref[begin + step]].astype(jnp.float32)
            value = raised[:, half * BS:(half + 1) * BS] * (keep * (1.0 / (lower + upper)))
            tiles[step] = value.astype(jnp.bfloat16)
            acc = acc + jnp.sum(value.reshape(BS // 8, 8, BS), axis=0)
        return acc

    def arrive(pair):
        slot = lax.rem(pair, BUFFERS)
        for half in range(2):
            pltpu.make_async_copy(dens.at[pl.ds(0, PAD), pl.ds(0, WIDE)],
                                  buf.at[slot, half], fetch_sem.at[slot, half]).wait()

    for ahead in range(min(BUFFERS - 1, pairs)):
        fetch(ahead, ahead)
    arrive(0)
    along_columns(0)

    def body(pair, acc):
        @pl.when(pair + BUFFERS - 2 < pairs)
        def _():
            fetch(pair + BUFFERS - 2, lax.rem(pair + BUFFERS - 2, BUFFERS))

        arrive(pair)
        acc = along_rows(pair - 1, acc)
        along_columns(pair)
        return acc

    acc = lax.fori_loop(1, pairs, body, acc_in[...])
    acc_out[...] = along_rows(pairs - 1, acc)

    stores = []
    for g in range(count):
        if has_local and g == count - 1:
            for r in range(capacity):
                slot = meta_ref[layout.place + (first + g) * capacity + r]
                stores.append(pltpu.make_async_copy(
                    tiles.at[g * capacity + r], outs[g].at[slot], store_sem.at[len(stores)]))
        else:
            stores.append(pltpu.make_async_copy(
                tiles.at[pl.ds(g * capacity, capacity)], outs[g], store_sem.at[len(stores)]))
    for store in stores:
        store.start()
    for store in stores:
        store.wait()


def project(meta, fields, acc, *, layout, first, count, block_rows, block_cols, has_local):
    capacity = layout.capacity
    block_count = block_rows * block_cols
    sent = jax.ShapeDtypeStruct((capacity, BS, BS), jnp.bfloat16)
    whole = jax.ShapeDtypeStruct((block_count, BS, BS), jnp.bfloat16)
    shapes = [sent] * count
    if has_local:
        shapes[-1] = whole
    anywhere = pl.BlockSpec(memory_space=pl.ANY)
    vmem = pl.BlockSpec(memory_space=pltpu.VMEM)
    kernel = functools.partial(
        project_kernel, layout=layout, first=first, count=count, block_rows=block_rows,
        block_cols=block_cols, has_local=has_local)
    steps = count * capacity
    results = pl.pallas_call(
        kernel,
        out_shape=tuple(shapes) + (jax.ShapeDtypeStruct((8, BS), jnp.float32),),
        in_specs=[pl.BlockSpec(memory_space=pltpu.SMEM)] + [anywhere] * 5 + [vmem] * 3,
        out_specs=tuple([anywhere] * count + [vmem]),
        scratch_shapes=[
            pltpu.VMEM((BUFFERS, 2, PAD, WIDE), jnp.float32),
            pltpu.SemaphoreType.DMA((BUFFERS, 2)),
            pltpu.VMEM((2, PAD, 2 * BS), jnp.bfloat16),
            pltpu.VMEM((steps, BS, BS), jnp.bfloat16),
            pltpu.SemaphoreType.DMA((count + capacity,)),
        ],
        cost_estimate=pl.CostEstimate(
            flops=steps * 300_000_000, bytes_accessed=steps * 300_000, transcendentals=0),
        name="project",
    )(meta, *fields, acc)
    return results[:-1], results[-1]


def place_kernel(meta_ref, out_in, *refs, layout, first, count, parts):
    del out_in
    arrived, refs = refs[:count], refs[count:]
    addends, refs = refs[:parts], refs[parts:]
    out, sem = refs[0], refs[-1]
    capacity = layout.capacity
    for g in range(count):
        for r in range(capacity):
            slot = meta_ref[layout.place + (first + g) * capacity + r]
            pltpu.make_async_copy(arrived[g].at[r], out.at[slot], sem).start()
    if parts:
        refs[1][...] = pairwise_sum([addend[...] for addend in addends])
    everything = out.at[pl.ds(0, count * capacity)]
    pltpu.make_async_copy(everything, everything, sem).wait()


def place(meta, out, arrived, addends, *, layout, first):
    anywhere = pl.BlockSpec(memory_space=pl.ANY)
    vmem = pl.BlockSpec(memory_space=pltpu.VMEM)
    shapes = [jax.ShapeDtypeStruct(out.shape, out.dtype)]
    shapes += [jax.ShapeDtypeStruct(a.shape, a.dtype) for a in addends[:1]]
    results = pl.pallas_call(
        functools.partial(place_kernel, layout=layout, first=first, count=len(arrived),
                          parts=len(addends)),
        out_shape=tuple(shapes),
        in_specs=[pl.BlockSpec(memory_space=pltpu.SMEM), anywhere]
        + [vmem] * (len(arrived) + len(addends)),
        out_specs=tuple([anywhere] + [vmem] * len(addends[:1])),
        scratch_shapes=[pltpu.SemaphoreType.DMA],
        input_output_aliases={1: 0},
        name="place",
    )(meta, out, *arrived, *addends)
    return results[0], results[-1]


def pairwise_sum(parts):
    while len(parts) > 1:
        parts = [a + b for a, b in zip(parts[::2], parts[1::2])]
    return parts[0]


def spread(value, axis):
    count = lax.axis_size(axis)
    parts = [value]
    for offset in range(1, count):
        parts.append(lax.ppermute(value, axis, [(i, i ^ offset) for i in range(count)]))
    return parts


def grouped(items, sizes):
    groups = []
    for size in sizes:
        if items:
            groups.append(items[:size])
            items = items[size:]
    return groups


def per_device(density, design_mask, rebalance):
    tile_rows, tile_cols = density.shape
    block_rows, block_cols = design_mask.shape
    block_count = block_rows * block_cols
    row_count = lax.axis_size("row")
    col_count = lax.axis_size("col")
    device_count = row_count * col_count
    capacity = block_count // device_count
    assert capacity * device_count == block_count and capacity % 2 == 0
    assert block_rows > 1 and block_cols > 1
    me = lax.axis_index(AXES)
    order = exchange_order(row_count, col_count) + [0]
    layout = Meta(device_count, capacity)
    top, bottom, left, right = with_halo(density)
    tables = block_tables(
        rebalance, me, block_rows, block_cols, row_count, col_count, capacity, order)
    meta = jnp.concatenate([tables, design_mask.reshape(-1)])
    fields = (density, top, bottom, left, right, *band_matrices())

    unit = max(1, 8 // capacity)
    groups = grouped(order, [unit * size for size in GROUPS])
    acc = jnp.zeros((8, BS), jnp.float32)
    arrivals, first = [], 0
    for group in groups:
        sent, acc = project(
            meta, fields, acc, layout=layout, first=first, count=len(group),
            block_rows=block_rows, block_cols=block_cols, has_local=group[-1] == 0)
        for offset, part in zip(group, sent):
            if offset:
                pairs = [(i, i ^ offset) for i in range(device_count)]
                arrivals.append(lax.ppermute(part, AXES, pairs))
            else:
                out = part
        first += len(group)

    tail = [2 * unit, 1 * unit]
    bulk = len(arrivals) - sum(tail)
    sizes = [bulk % (4 * unit)] + [4 * unit] * (bulk // (4 * unit)) + tail
    sizes = [size for size in sizes if size]
    begin = 0
    addends = spread(acc, "row")
    for index, size in enumerate(sizes):
        now = addends if index in (len(sizes) // 2, len(sizes) - 1) else []
        out, total = place(meta, out, arrivals[begin:begin + size], now,
                           layout=layout, first=begin)
        if index == len(sizes) // 2:
            addends = spread(total, "col")
        begin += size
    grid_cells = float(tile_rows * tile_cols * device_count)
    constraint = jnp.sum(total) / grid_cells / VOLUME_TARGET - 1.0
    return out, constraint


def solution(mesh):
    return jax.shard_map(
        per_device,
        mesh=mesh,
        in_specs=(P("row", "col"), P("row", "col"), P()),
        out_specs=(P(AXES, None, None), P()),
        check_vma=False,
    )
```

profile of v0, /device:TPU:0, one launch (start us, length us, event | category | flops | bytes accessed | tf_op | source)
XLA Modules:
  0.0 327.0 jit_solution(8999064807636455416)
XLA Ops:
  1.7 1.3 collective-permute-start.1
  3.0 3.0 collective-permute-start
  10.4 1.4 fusion.10
  13.3 1.3 collective-permute-start.3
  14.9 5.5 %collective-permute-start.2 = (f32[16,1056]{1,0:T(8,128)S(1)}, f32[16,1056]{1,0:T(8,128)S(1)}, u32[]{:S(2)}, u32[]{:S(2)}) collective-permute-start(f32[16,1056]{1,0:T(8,128)S(1)} %concatenate.18), channel_id=1, source_target_pairs={{0,1},{1,2},{2,3},{3,4},{4,5},{5,6},{6,7},{8,9},{9,10},{10,11},{11... | collective-permute-start | bytes 202760 | tf_op jit(solution)/shard_map/ppermute | solution.py:90
  21.7 1.5 collective-permute-done.2
  25.1 7.2 %project.5 = (bf16[8,128,128]{2,1,0:T(8,128)(2,1)}, bf16[8,128,128]{2,1,0:T(8,128)(2,1)}, f32[8,128]{1,0:T(8,128)}) custom-call(s32[768]{0:T(1024)} %copy-done, f32[1024,4096]{1,0:T(8,128)} %dens.9, f32[16,4096]{1,0:T(8,128)} %copy-done.2, f32[16,4096]{1,0:T(8,128)} %copy-done.1, f32[1056,128]{1,0:T(8,128)} %pad_bitcast_fusion.1.left, ...), custom_call_target="tpu_custom_call" | custom-call | flops 4800000000 | bytes 4800000 | tf_op jit(solution)/shard_map/project/pallas_call | solution.py:287
  32.3 5.7 %collective-permute-start.4 = (bf16[8,128,128]{2,1,0:T(8,128)(2,1)}, bf16[8,128,128]{2,1,0:T(8,128)(2,1)S(1)}, u32[]{:S(2)}, u32[]{:S(2)}) collective-permute-start(bf16[8,128,128]{2,1,0:T(8,128)(2,1)} %get-tuple-element.48), channel_id=1, source_target_pairs={{0,4},{1,5},{2,6},{3,7},{4,0},{5,1},{6,2},{7,3},{8,12},{9,13},{10,... | collective-permute-start | bytes 786440 | tf_op jit(solution)/shard_map/ppermute | solution.py:394
  38.0 11.1 %project.6 = (bf16[8,128,128]{2,1,0:T(8,128)(2,1)}, bf16[8,128,128]{2,1,0:T(8,128)(2,1)}, bf16[8,128,128]{2,1,0:T(8,128)(2,1)}, bf16[8,128,128]{2,1,0:T(8,128)(2,1)}, f32[8,128]{1,0:T(8,128)}) custom-call(s32[768]{0:T(1024)} %copy-done, f32[1024,4096]{1,0:T(8,128)} %dens.9, f32[16,4096]{1,0:T(8,128)} %copy-done.2, f32[16,4096]{1,0:T(8,128)} %copy-done.1, ...), custom_call_target="tpu_custom_call" | custom-call | flops 9600000000 | bytes 9600000 | tf_op jit(solution)/shard_map/project/pallas_call | solution.py:287
  49.1 18.9 %project.7 = (bf16[8,128,128]{2,1,0:T(8,128)(2,1)}, bf16[8,128,128]{2,1,0:T(8,128)(2,1)}, bf16[8,128,128]{2,1,0:T(8,128)(2,1)}, bf16[8,128,128]{2,1,0:T(8,128)(2...) custom-call(s32[768]{0:T(1024)} %copy-done, ...), custom_call_target="tpu_custom_call" | custom-call | flops 19200000000 | bytes 19200000 | tf_op jit(solution)/shard_map/project/pallas_call | solution.py:287
  68.0 18.9 %project.8 = (bf16[8,128,128]{2,1,0:T(8,128)(2,1)}, bf16[8,128,128]{2,1,0:T(8,128)(2,1)}, bf16[8,128,128]{2,1,0:T(8,128)(2,1)}, bf16[8,128,128]{2,1,0:T(8,128)(2...) custom-call(s32[768]{0:T(1024)} %copy-done, ...), custom_call_target="tpu_custom_call" | custom-call | flops 19200000000 | bytes 19200000 | tf_op jit(solution)/shard_map/project/pallas_call | solution.py:287
  87.0 22.9 %project.9 = (bf16[8,128,128]{2,1,0:T(8,128)(2,1)}, bf16[8,128,128]{2,1,0:T(8,128)(2,1)}, bf16[8,128,128]{2,1,0:T(8,128)(2,1)}, bf16[8,128,128]{2,1,0:T(8,128)(2...) custom-call(s32[768]{0:T(1024)} %copy-done, ...), custom_call_target="tpu_custom_call" | custom-call | flops 24000000000 | bytes 24000000 | tf_op jit(solution)/shard_map/project/pallas_call | solution.py:287
  110.0 1.3 collective-permute-start.25
  113.2 1.5 collective-permute-start.6
  114.9 3.1 collective-permute-start.8
  118.9 4.0 %collective-permute-done.5.refs_1_ = bf16[8,128,128]{2,1,0:T(8,128)(2,1)S(1)} collective-permute-done((bf16[8,128,128]{2,1,0:T(8,128)(2,1)S(1)}, bf16[8,128,128]{2,1,0:T(8,128)(2,1)S(1)}, u32[]{:S(2)}, u32[]{:S(2)}) %collective-permute-start.5) | collective-permute-done | bytes 262176 | tf_op jit(solution)/shard_map/ppermute | solution.py:394
  122.9 5.4 %collective-permute-start.10 = (bf16[8,128,128]{2,1,0:T(8,128)(2,1)S(1)}, bf16[8,128,128]{2,1,0:T(8,128)(2,1)S(1)}, u32[]{:S(2)}, u32[]{:S(2)}) collective-permute-start(bf16[8,128,128]{2,1,0:T(8,128)(2,1)S(1)} %copy-done.35), channel_id=1, source_target_pairs={{0,3},{1,2},{2,1},{3,0},{4,7},{5,6},{6,5},{7,4},{8,11},{9,10},{10,... | collective-permute-start | bytes 786440 | tf_op jit(solution)/shard_map/ppermute | solution.py:394
  129.2 15.4 %collective-permute-done.8.refs_0_ = bf16[8,128,128]{2,1,0:T(8,128)(2,1)S(1)} collective-permute-done((bf16[8,128,128]{2,1,0:T(8,128)(2,1)S(1)}, bf16[8,128,128]{2,1,0:T(8,128)(2,1)S(1)}, u32[]{:S(2)}, u32[]{:S(2)}) %collective-permute-start.8) | collective-permute-done | bytes 262176 | tf_op jit(solution)/shard_map/ppermute | solution.py:394
  144.6 14.4 %collective-permute-start.14 = (bf16[8,128,128]{2,1,0:T(8,128)(2,1)}, bf16[8,128,128]{2,1,0:T(8,128)(2,1)S(1)}, u32[]{:S(2)}, u32[]{:S(2)}) collective-permute-start(bf16[8,128,128]{2,1,0:T(8,128)(2,1)} %get-tuple-element.58), channel_id=1, source_target_pairs={{0,10},{1,11},{2,8},{3,9},{4,14},{5,15},{6,12},{7,13},{8,2},{9,3},... | collective-permute-start | bytes 786440 | tf_op jit(solution)/shard_map/ppermute | solution.py:394
  159.0 4.1 %collective-permute-start.15 = (bf16[8,128,128]{2,1,0:T(8,128)(2,1)}, bf16[8,128,128]{2,1,0:T(8,128)(2,1)S(1)}, u32[]{:S(2)}, u32[]{:S(2)}) collective-permute-start(bf16[8,128,128]{2,1,0:T(8,128)(2,1)} %get-tuple-element.59), channel_id=1, source_target_pairs={{0,9},{1,8},{2,11},{3,10},{4,13},{5,12},{6,15},{7,14},{8,1},{9,0},... | collective-permute-start | bytes 786440 | tf_op jit(solution)/shard_map/ppermute | solution.py:394
  163.1 2.1 collective-permute-done.12.refs_0_
  165.2 1.3 collective-permute-start.17
  166.6 16.5 %collective-permute-start.18 = (bf16[8,128,128]{2,1,0:T(8,128)(2,1)}, bf16[8,128,128]{2,1,0:T(8,128)(2,1)S(1)}, u32[]{:S(2)}, u32[]{:S(2)}) collective-permute-start(bf16[8,128,128]{2,1,0:T(8,128)(2,1)} %get-tuple-element.62), channel_id=1, source_target_pairs={{0,11},{1,10},{2,9},{3,8},{4,15},{5,14},{6,13},{7,12},{8,3},{9,2},... | collective-permute-start | bytes 786440 | tf_op jit(solution)/shard_map/ppermute | solution.py:394
  185.1 1.9 collective-permute-done.16.refs_0_
  187.0 1.7 collective-permute-start.21
  188.7 16.2 %collective-permute-start.22 = (bf16[8,128,128]{2,1,0:T(8,128)(2,1)}, bf16[8,128,128]{2,1,0:T(8,128)(2,1)S(1)}, u32[]{:S(2)}, u32[]{:S(2)}) collective-permute-start(bf16[8,128,128]{2,1,0:T(8,128)(2,1)} %get-tuple-element.66), channel_id=1, source_target_pairs={{0,18},{1,19},{2,16},{3,17},{4,22},{5,23},{6,20},{7,21},{8,26},{9,... | collective-permute-start | bytes 786440 | tf_op jit(solution)/shard_map/ppermute | solution.py:394
  204.9 3.2 collective-permute-start.23
  209.2 5.0 %collective-permute-done.20.refs_0_ = bf16[8,128,128]{2,1,0:T(8,128)(2,1)S(1)} collective-permute-done((bf16[8,128,128]{2,1,0:T(8,128)(2,1)}, bf16[8,128,128]{2,1,0:T(8,128)(2,1)S(1)}, u32[]{:S(2)}, u32[]{:S(2)}) %collective-permute-start.20) | collective-permute-done | bytes 262176 | tf_op jit(solution)/shard_map/ppermute | solution.py:394
  214.1 1.8 collective-permute-start.28
  216.0 21.1 %collective-permute-start.29 = (bf16[8,128,128]{2,1,0:T(8,128)(2,1)}, bf16[8,128,128]{2,1,0:T(8,128)(2,1)}, u32[]{:S(2)}, u32[]{:S(2)}) collective-permute-start(bf16[8,128,128]{2,1,0:T(8,128)(2,1)} %get-tuple-element.72), channel_id=1, source_target_pairs={{0,19},{1,18},{2,17},{3,16},{4,23},{5,22},{6,21},{7,20},{8,27},{9,... | collective-permute-start | bytes 786440 | tf_op jit(solution)/shard_map/ppermute | solution.py:394
  237.2 4.8 %collective-permute-done.27.refs_0_ = bf16[8,128,128]{2,1,0:T(8,128)(2,1)S(1)} collective-permute-done((bf16[8,128,128]{2,1,0:T(8,128)(2,1)}, bf16[8,128,128]{2,1,0:T(8,128)(2,1)S(1)}, u32[]{:S(2)}, u32[]{:S(2)}) %collective-permute-start.27) | collective-permute-done | bytes 262176 | tf_op jit(solution)/shard_map/ppermute | solution.py:394
  243.1 15.4 %collective-permute-start.33 = (bf16[8,128,128]{2,1,0:T(8,128)(2,1)}, bf16[8,128,128]{2,1,0:T(8,128)(2,1)}, u32[]{:S(2)}, u32[]{:S(2)}) collective-permute-start(bf16[8,128,128]{2,1,0:T(8,128)(2,1)} %get-tuple-element.76), channel_id=1, source_target_pairs={{0,26},{1,27},{2,24},{3,25},{4,30},{5,31},{6,28},{7,29},{8,18},{9,... | collective-permute-start | bytes 786440 | tf_op jit(solution)/shard_map/ppermute | solution.py:394
  258.5 5.3 %collective-permute-start.34 = (bf16[8,128,128]{2,1,0:T(8,128)(2,1)}, bf16[8,128,128]{2,1,0:T(8,128)(2,1)}, u32[]{:S(2)}, u32[]{:S(2)}) collective-permute-start(bf16[8,128,128]{2,1,0:T(8,128)(2,1)} %get-tuple-element.77), channel_id=1, source_target_pairs={{0,25},{1,24},{2,27},{3,26},{4,29},{5,28},{6,31},{7,30},{8,17},{9,... | collective-permute-start | bytes 786440 | tf_op jit(solution)/shard_map/ppermute | solution.py:394
  263.9 14.0 %collective-permute-start.35 = (bf16[8,128,128]{2,1,0:T(8,128)(2,1)}, bf16[8,128,128]{2,1,0:T(8,128)(2,1)}, u32[]{:S(2)}, u32[]{:S(2)}) collective-permute-start(bf16[8,128,128]{2,1,0:T(8,128)(2,1)} %get-tuple-element.78), channel_id=1, source_target_pairs={{0,29},{1,28},{2,31},{3,30},{4,25},{5,24},{6,27},{7,26},{8,21},{9,... | collective-permute-start | bytes 786440 | tf_op jit(solution)/shard_map/ppermute | solution.py:394
  277.9 2.2 collective-permute-start.37
  280.0 2.2 place.9.out_in
  282.3 2.2 place.10.out_in
  284.5 2.2 place.11.out_in
  286.6 2.2 place.12.out_in
  288.8 2.8 place.13
  291.6 3.3 collective-permute-start.44
  294.8 13.5 %collective-permute-start.43 = (f32[8,128]{1,0:T(8,128)}, f32[8,128]{1,0:T(8,128)S(1)}, u32[]{:S(2)}, u32[]{:S(2)}) collective-permute-start(f32[8,128]{1,0:T(8,128)} %get-tuple-element.81.refs_1_), channel_id=1, source_target_pairs={{0,6},{1,7},{2,4},{3,5},{4,2},{5,3},{6,0},{7,1},{8,14},{9,15},{10,... | collective-permute-start | bytes 12296 | tf_op jit(solution)/shard_map/ppermute | solution.py:351
  308.5 1.5 collective-permute-start.40
  310.0 4.2 %collective-permute-start.39 = (f32[8,128]{1,0:T(8,128)}, f32[8,128]{1,0:T(8,128)S(1)}, u32[]{:S(2)}, u32[]{:S(2)}) collective-permute-start(f32[8,128]{1,0:T(8,128)} %get-tuple-element.81.refs_1_), channel_id=1, source_target_pairs={{0,2},{1,3},{2,0},{3,1},{4,6},{5,7},{6,4},{7,5},{8,10},{9,11},{10,... | collective-permute-start | bytes 12296 | tf_op jit(solution)/shard_map/ppermute | solution.py:351
  314.2 2.2 place.14.out_in
  316.4 2.2 place.15.out_in
  318.6 1.8 place.16.out_in
  321.7 2.3 place.17
  (174 shorter events, 21.0 us)
Async XLA Ops:
  1.7 11.2 %collective-permute-start.1 = (f32[16,4096]{1,0:T(8,128)S(1)}, f32[16,4096]{1,0:T(8,128)S(1)}, u32[]{:S(2)}, u32[]{:S(2)}) collective-permute-start(f32[16,4096]{1,0:T(8,128)S(1)} %get-tuple-element.88), channel_id=1, source_target_pairs={{8,0},{16,8},{24,16},{9,1},{17,9},{25,17},{10,2},{18,10},{26,18},{... | collective-permute-start | bytes 786440 | tf_op jit(solution)/shard_map/ppermute | solution.py:83
  3.0 10.1 %collective-permute-start = (f32[16,4096]{1,0:T(8,128)S(1)}, f32[16,4096]{1,0:T(8,128)S(1)}, u32[]{:S(2)}, u32[]{:S(2)}) collective-permute-start(f32[16,4096]{1,0:T(8,128)S(1)} %get-tuple-element.89), channel_id=1, source_target_pairs={{0,8},{8,16},{16,24},{1,9},{9,17},{17,25},{2,10},{10,18},{18,26},{... | collective-permute-start | bytes 786440 | tf_op jit(solution)/shard_map/ppermute | solution.py:82
  13.3 7.3 %collective-permute-start.3 = (f32[16,1056]{1,0:T(8,128)S(1)}, f32[16,1056]{1,0:T(8,128)S(1)}, u32[]{:S(2)}, u32[]{:S(2)}) collective-permute-start(f32[16,1056]{1,0:T(8,128)S(1)} %concatenate.19), channel_id=1, source_target_pairs={{1,0},{2,1},{3,2},{4,3},{5,4},{6,5},{7,6},{9,8},{10,9},{11,10},{12... | collective-permute-start | bytes 202760 | tf_op jit(solution)/shard_map/ppermute | solution.py:91
  14.9 8.3 %collective-permute-start.2 = (f32[16,1056]{1,0:T(8,128)S(1)}, f32[16,1056]{1,0:T(8,128)S(1)}, u32[]{:S(2)}, u32[]{:S(2)}) collective-permute-start(f32[16,1056]{1,0:T(8,128)S(1)} %concatenate.18), channel_id=1, source_target_pairs={{0,1},{1,2},{2,3},{3,4},{4,5},{5,6},{6,7},{8,9},{9,10},{10,11},{11... | collective-permute-start | bytes 202760 | tf_op jit(solution)/shard_map/ppermute | solution.py:90
  32.3 85.7 %collective-permute-start.4 = (bf16[8,128,128]{2,1,0:T(8,128)(2,1)}, bf16[8,128,128]{2,1,0:T(8,128)(2,1)S(1)}, u32[]{:S(2)}, u32[]{:S(2)}) collective-permute-start(bf16[8,128,128]{2,1,0:T(8,128)(2,1)} %get-tuple-element.48), channel_id=1, source_target_pairs={{0,4},{1,5},{2,6},{3,7},{4,0},{5,1},{6,2},{7,3},{8,12},{9,13},{10,... | collective-permute-start | bytes 786440 | tf_op jit(solution)/shard_map/ppermute | solution.py:394
  109.9 3.3 %collective-permute-start.26 = (f32[8,128]{1,0:T(8,128)}, f32[8,128]{1,0:T(8,128)S(1)}, u32[]{:S(2)}, u32[]{:S(2)}) collective-permute-start(f32[8,128]{1,0:T(8,128)} %get-tuple-element.68.refs_4_), channel_id=1, source_target_pairs={{0,24},{8,16},{16,8},{24,0},{1,25},{9,17},{17,9},{25,1},{2,26},{10... | collective-permute-start | bytes 12296 | tf_op jit(solution)/shard_map/ppermute | solution.py:351
  110.0 4.7 %collective-permute-start.25 = (f32[8,128]{1,0:T(8,128)}, f32[8,128]{1,0:T(8,128)S(1)}, u32[]{:S(2)}, u32[]{:S(2)}) collective-permute-start(f32[8,128]{1,0:T(8,128)} %get-tuple-element.68.refs_4_), channel_id=1, source_target_pairs={{0,16},{8,24},{16,0},{24,8},{1,17},{9,25},{17,1},{25,9},{2,18},{10... | collective-permute-start | bytes 12296 | tf_op jit(solution)/shard_map/ppermute | solution.py:351
  111.3 3.5 %collective-permute-start.24 = (f32[8,128]{1,0:T(8,128)}, f32[8,128]{1,0:T(8,128)S(1)}, u32[]{:S(2)}, u32[]{:S(2)}) collective-permute-start(f32[8,128]{1,0:T(8,128)} %get-tuple-element.68.refs_4_), channel_id=1, source_target_pairs={{0,8},{8,0},{16,24},{24,16},{1,9},{9,1},{17,25},{25,17},{2,10},{10... | collective-permute-start | bytes 12296 | tf_op jit(solution)/shard_map/ppermute | solution.py:351
  111.9 11.0 %collective-permute-start.5 = (bf16[8,128,128]{2,1,0:T(8,128)(2,1)S(1)}, bf16[8,128,128]{2,1,0:T(8,128)(2,1)S(1)}, u32[]{:S(2)}, u32[]{:S(2)}) collective-permute-start(bf16[8,128,128]{2,1,0:T(8,128)(2,1)S(1)} %copy-done.39), channel_id=1, source_target_pairs={{0,6},{1,7},{2,4},{3,5},{4,2},{5,3},{6,0},{7,1},{8,14},{9,15},{10,... | collective-permute-start | bytes 786440 | tf_op jit(solution)/shard_map/ppermute | solution.py:394
  113.2 168.9 %copy-start.24 = (f32[8,128]{1,0:T(8,128)}, f32[8,128]{1,0:T(8,128)S(1)}, u32[]{:S(2)}) copy-start(f32[8,128]{1,0:T(8,128)S(1)} %collective-permute-done.26.refs_7_) | copy-start | bytes 12292
  113.2 15.0 %collective-permute-start.6 = (bf16[8,128,128]{2,1,0:T(8,128)(2,1)S(1)}, bf16[8,128,128]{2,1,0:T(8,128)(2,1)S(1)}, u32[]{:S(2)}, u32[]{:S(2)}) collective-permute-start(bf16[8,128,128]{2,1,0:T(8,128)(2,1)S(1)} %copy-done.40), channel_id=1, source_target_pairs={{0,2},{1,3},{2,0},{3,1},{4,6},{5,7},{6,4},{7,5},{8,10},{9,11},{10,... | collective-permute-start | bytes 786440 | tf_op jit(solution)/shard_map/ppermute | solution.py:394
  114.8 167.4 %copy-start.25 = (f32[8,128]{1,0:T(8,128)}, f32[8,128]{1,0:T(8,128)S(1)}, u32[]{:S(2)}) copy-start(f32[8,128]{1,0:T(8,128)S(1)} %collective-permute-done.25.refs_6_) | copy-start | bytes 12292
  114.8 13.5 %collective-permute-start.7 = (bf16[8,128,128]{2,1,0:T(8,128)(2,1)S(1)}, bf16[8,128,128]{2,1,0:T(8,128)(2,1)S(1)}, u32[]{:S(2)}, u32[]{:S(2)}) collective-permute-start(bf16[8,128,128]{2,1,0:T(8,128)(2,1)S(1)} %copy-done.38), channel_id=1, source_target_pairs={{0,1},{1,0},{2,3},{3,2},{4,5},{5,4},{6,7},{7,6},{8,9},{9,8},{10,11... | collective-permute-start | bytes 786440 | tf_op jit(solution)/shard_map/ppermute | solution.py:394
  114.8 167.4 %copy-start.26 = (f32[8,128]{1,0:T(8,128)}, f32[8,128]{1,0:T(8,128)S(1)}, u32[]{:S(2)}) copy-start(f32[8,128]{1,0:T(8,128)S(1)} %collective-permute-done.24.refs_5_) | copy-start | bytes 12292
  114.9 29.7 %collective-permute-start.8 = (bf16[8,128,128]{2,1,0:T(8,128)(2,1)S(1)}, bf16[8,128,128]{2,1,0:T(8,128)(2,1)S(1)}, u32[]{:S(2)}, u32[]{:S(2)}) collective-permute-start(bf16[8,128,128]{2,1,0:T(8,128)(2,1)S(1)} %copy-done.37), channel_id=1, source_target_pairs={{0,5},{1,4},{2,7},{3,6},{4,1},{5,0},{6,3},{7,2},{8,13},{9,12},{10,... | collective-permute-start | bytes 786440 | tf_op jit(solution)/shard_map/ppermute | solution.py:394
  117.9 26.7 %collective-permute-start.9 = (bf16[8,128,128]{2,1,0:T(8,128)(2,1)S(1)}, bf16[8,128,128]{2,1,0:T(8,128)(2,1)S(1)}, u32[]{:S(2)}, u32[]{:S(2)}) collective-permute-start(bf16[8,128,128]{2,1,0:T(8,128)(2,1)S(1)} %copy-done.36), channel_id=1, source_target_pairs={{0,7},{1,6},{2,5},{3,4},{4,3},{5,2},{6,1},{7,0},{8,15},{9,14},{10,... | collective-permute-start | bytes 786440 | tf_op jit(solution)/shard_map/ppermute | solution.py:394
  122.9 36.1 %collective-permute-start.10 = (bf16[8,128,128]{2,1,0:T(8,128)(2,1)S(1)}, bf16[8,128,128]{2,1,0:T(8,128)(2,1)S(1)}, u32[]{:S(2)}, u32[]{:S(2)}) collective-permute-start(bf16[8,128,128]{2,1,0:T(8,128)(2,1)S(1)} %copy-done.35), channel_id=1, source_target_pairs={{0,3},{1,2},{2,1},{3,0},{4,7},{5,6},{6,5},{7,4},{8,11},{9,10},{10,... | collective-permute-start | bytes 786440 | tf_op jit(solution)/shard_map/ppermute | solution.py:394
  128.3 34.8 %collective-permute-start.11 = (bf16[8,128,128]{2,1,0:T(8,128)(2,1)}, bf16[8,128,128]{2,1,0:T(8,128)(2,1)S(1)}, u32[]{:S(2)}, u32[]{:S(2)}) collective-permute-start(bf16[8,128,128]{2,1,0:T(8,128)(2,1)} %get-tuple-element.55), channel_id=1, source_target_pairs={{0,8},{1,9},{2,10},{3,11},{4,12},{5,13},{6,14},{7,15},{8,0},{9,1},... | collective-permute-start | bytes 786440 | tf_op jit(solution)/shard_map/ppermute | solution.py:394
  128.3 36.9 %collective-permute-start.12 = (bf16[8,128,128]{2,1,0:T(8,128)(2,1)}, bf16[8,128,128]{2,1,0:T(8,128)(2,1)S(1)}, u32[]{:S(2)}, u32[]{:S(2)}) collective-permute-start(bf16[8,128,128]{2,1,0:T(8,128)(2,1)} %get-tuple-element.56), channel_id=1, source_target_pairs={{0,12},{1,13},{2,14},{3,15},{4,8},{5,9},{6,10},{7,11},{8,4},{9,5},... | collective-permute-start | bytes 786440 | tf_op jit(solution)/shard_map/ppermute | solution.py:394
  144.6 22.0 %collective-permute-start.13 = (bf16[8,128,128]{2,1,0:T(8,128)(2,1)}, bf16[8,128,128]{2,1,0:T(8,128)(2,1)S(1)}, u32[]{:S(2)}, u32[]{:S(2)}) collective-permute-start(bf16[8,128,128]{2,1,0:T(8,128)(2,1)} %get-tuple-element.57), channel_id=1, source_target_pairs={{0,14},{1,15},{2,12},{3,13},{4,10},{5,11},{6,8},{7,9},{8,6},{9,7},... | collective-permute-start | bytes 786440 | tf_op jit(solution)/shard_map/ppermute | solution.py:394
  144.6 38.5 %collective-permute-start.14 = (bf16[8,128,128]{2,1,0:T(8,128)(2,1)}, bf16[8,128,128]{2,1,0:T(8,128)(2,1)S(1)}, u32[]{:S(2)}, u32[]{:S(2)}) collective-permute-start(bf16[8,128,128]{2,1,0:T(8,128)(2,1)} %get-tuple-element.58), channel_id=1, source_target_pairs={{0,10},{1,11},{2,8},{3,9},{4,14},{5,15},{6,12},{7,13},{8,2},{9,3},... | collective-permute-start | bytes 786440 | tf_op jit(solution)/shard_map/ppermute | solution.py:394
  159.0 24.9 %collective-permute-start.15 = (bf16[8,128,128]{2,1,0:T(8,128)(2,1)}, bf16[8,128,128]{2,1,0:T(8,128)(2,1)S(1)}, u32[]{:S(2)}, u32[]{:S(2)}) collective-permute-start(bf16[8,128,128]{2,1,0:T(8,128)(2,1)} %get-tuple-element.59), channel_id=1, source_target_pairs={{0,9},{1,8},{2,11},{3,10},{4,13},{5,12},{6,15},{7,14},{8,1},{9,0},... | collective-permute-start | bytes 786440 | tf_op jit(solution)/shard_map/ppermute | solution.py:394
  163.1 23.9 %collective-permute-start.16 = (bf16[8,128,128]{2,1,0:T(8,128)(2,1)}, bf16[8,128,128]{2,1,0:T(8,128)(2,1)S(1)}, u32[]{:S(2)}, u32[]{:S(2)}) collective-permute-start(bf16[8,128,128]{2,1,0:T(8,128)(2,1)} %get-tuple-element.60), channel_id=1, source_target_pairs={{0,13},{1,12},{2,15},{3,14},{4,9},{5,8},{6,11},{7,10},{8,5},{9,4},... | collective-permute-start | bytes 786440 | tf_op jit(solution)/shard_map/ppermute | solution.py:394
  165.2 23.4 %collective-permute-start.17 = (bf16[8,128,128]{2,1,0:T(8,128)(2,1)}, bf16[8,128,128]{2,1,0:T(8,128)(2,1)S(1)}, u32[]{:S(2)}, u32[]{:S(2)}) collective-permute-start(bf16[8,128,128]{2,1,0:T(8,128)(2,1)} %get-tuple-element.61), channel_id=1, source_target_pairs={{0,15},{1,14},{2,13},{3,12},{4,11},{5,10},{6,9},{7,8},{8,7},{9,6},... | collective-permute-start | bytes 786440 | tf_op jit(solution)/shard_map/ppermute | solution.py:394
  166.6 38.3 %collective-permute-start.18 = (bf16[8,128,128]{2,1,0:T(8,128)(2,1)}, bf16[8,128,128]{2,1,0:T(8,128)(2,1)S(1)}, u32[]{:S(2)}, u32[]{:S(2)}) collective-permute-start(bf16[8,128,128]{2,1,0:T(8,128)(2,1)} %get-tuple-element.62), channel_id=1, source_target_pairs={{0,11},{1,10},{2,9},{3,8},{4,15},{5,14},{6,13},{7,12},{8,3},{9,2},... | collective-permute-start | bytes 786440 | tf_op jit(solution)/shard_map/ppermute | solution.py:394
  183.1 25.0 %collective-permute-start.19 = (bf16[8,128,128]{2,1,0:T(8,128)(2,1)S(1)}, bf16[8,128,128]{2,1,0:T(8,128)(2,1)S(1)}, u32[]{:S(2)}, u32[]{:S(2)}) collective-permute-start(bf16[8,128,128]{2,1,0:T(8,128)(2,1)S(1)} %copy-done.34), channel_id=1, source_target_pairs={{0,16},{1,17},{2,18},{3,19},{4,20},{5,21},{6,22},{7,23},{8,24},{9,... | collective-permute-start | bytes 786440 | tf_op jit(solution)/shard_map/ppermute | solution.py:394
  184.0 30.2 %collective-permute-start.20 = (bf16[8,128,128]{2,1,0:T(8,128)(2,1)}, bf16[8,128,128]{2,1,0:T(8,128)(2,1)S(1)}, u32[]{:S(2)}, u32[]{:S(2)}) collective-permute-start(bf16[8,128,128]{2,1,0:T(8,128)(2,1)} %get-tuple-element.64), channel_id=1, source_target_pairs={{0,20},{1,21},{2,22},{3,23},{4,16},{5,17},{6,18},{7,19},{8,28},{9,... | collective-permute-start | bytes 786440 | tf_op jit(solution)/shard_map/ppermute | solution.py:394
  187.0 29.0 %collective-permute-start.21 = (bf16[8,128,128]{2,1,0:T(8,128)(2,1)}, bf16[8,128,128]{2,1,0:T(8,128)(2,1)S(1)}, u32[]{:S(2)}, u32[]{:S(2)}) collective-permute-start(bf16[8,128,128]{2,1,0:T(8,128)(2,1)} %get-tuple-element.65), channel_id=1, source_target_pairs={{0,22},{1,23},{2,20},{3,21},{4,18},{5,19},{6,16},{7,17},{8,30},{9,... | collective-permute-start | bytes 786440 | tf_op jit(solution)/shard_map/ppermute | solution.py:394
  188.7 48.4 %collective-permute-start.22 = (bf16[8,128,128]{2,1,0:T(8,128)(2,1)}, bf16[8,128,128]{2,1,0:T(8,128)(2,1)S(1)}, u32[]{:S(2)}, u32[]{:S(2)}) collective-permute-start(bf16[8,128,128]{2,1,0:T(8,128)(2,1)} %get-tuple-element.66), channel_id=1, source_target_pairs={{0,18},{1,19},{2,16},{3,17},{4,22},{5,23},{6,20},{7,21},{8,26},{9,... | collective-permute-start | bytes 786440 | tf_op jit(solution)/shard_map/ppermute | solution.py:394
  204.9 32.2 %collective-permute-start.23 = (bf16[8,128,128]{2,1,0:T(8,128)(2,1)}, bf16[8,128,128]{2,1,0:T(8,128)(2,1)S(1)}, u32[]{:S(2)}, u32[]{:S(2)}) collective-permute-start(bf16[8,128,128]{2,1,0:T(8,128)(2,1)} %get-tuple-element.67), channel_id=1, source_target_pairs={{0,17},{1,16},{2,19},{3,18},{4,21},{5,20},{6,23},{7,22},{8,25},{9,... | collective-permute-start | bytes 786440 | tf_op jit(solution)/shard_map/ppermute | solution.py:394
  208.1 33.8 %collective-permute-start.27 = (bf16[8,128,128]{2,1,0:T(8,128)(2,1)}, bf16[8,128,128]{2,1,0:T(8,128)(2,1)S(1)}, u32[]{:S(2)}, u32[]{:S(2)}) collective-permute-start(bf16[8,128,128]{2,1,0:T(8,128)(2,1)} %get-tuple-element.70), channel_id=1, source_target_pairs={{0,21},{1,20},{2,23},{3,22},{4,17},{5,16},{6,19},{7,18},{8,29},{9,... | collective-permute-start | bytes 786440 | tf_op jit(solution)/shard_map/ppermute | solution.py:394
  214.1 29.0 %collective-permute-start.28 = (bf16[8,128,128]{2,1,0:T(8,128)(2,1)}, bf16[8,128,128]{2,1,0:T(8,128)(2,1)}, u32[]{:S(2)}, u32[]{:S(2)}) collective-permute-start(bf16[8,128,128]{2,1,0:T(8,128)(2,1)} %get-tuple-element.71), channel_id=1, source_target_pairs={{0,23},{1,22},{2,21},{3,20},{4,19},{5,18},{6,17},{7,16},{8,31},{9,... | collective-permute-start | bytes 786440 | tf_op jit(solution)/shard_map/ppermute | solution.py:394
  216.0 42.6 %collective-permute-start.29 = (bf16[8,128,128]{2,1,0:T(8,128)(2,1)}, bf16[8,128,128]{2,1,0:T(8,128)(2,1)}, u32[]{:S(2)}, u32[]{:S(2)}) collective-permute-start(bf16[8,128,128]{2,1,0:T(8,128)(2,1)} %get-tuple-element.72), channel_id=1, source_target_pairs={{0,19},{1,18},{2,17},{3,16},{4,23},{5,22},{6,21},{7,20},{8,27},{9,... | collective-permute-start | bytes 786440 | tf_op jit(solution)/shard_map/ppermute | solution.py:394
  237.1 26.8 %collective-permute-start.30 = (bf16[8,128,128]{2,1,0:T(8,128)(2,1)}, bf16[8,128,128]{2,1,0:T(8,128)(2,1)}, u32[]{:S(2)}, u32[]{:S(2)}) collective-permute-start(bf16[8,128,128]{2,1,0:T(8,128)(2,1)} %get-tuple-element.73), channel_id=1, source_target_pairs={{0,24},{1,25},{2,26},{3,27},{4,28},{5,29},{6,30},{7,31},{8,16},{9,... | collective-permute-start | bytes 786440 | tf_op jit(solution)/shard_map/ppermute | solution.py:394
  237.1 40.7 %collective-permute-start.31 = (bf16[8,128,128]{2,1,0:T(8,128)(2,1)}, bf16[8,128,128]{2,1,0:T(8,128)(2,1)}, u32[]{:S(2)}, u32[]{:S(2)}) collective-permute-start(bf16[8,128,128]{2,1,0:T(8,128)(2,1)} %get-tuple-element.74), channel_id=1, source_target_pairs={{0,28},{1,29},{2,30},{3,31},{4,24},{5,25},{6,26},{7,27},{8,20},{9,... | collective-permute-start | bytes 786440 | tf_op jit(solution)/shard_map/ppermute | solution.py:394
  241.9 35.9 %collective-permute-start.32 = (bf16[8,128,128]{2,1,0:T(8,128)(2,1)}, bf16[8,128,128]{2,1,0:T(8,128)(2,1)}, u32[]{:S(2)}, u32[]{:S(2)}) collective-permute-start(bf16[8,128,128]{2,1,0:T(8,128)(2,1)} %get-tuple-element.75), channel_id=1, source_target_pairs={{0,30},{1,31},{2,28},{3,29},{4,26},{5,27},{6,24},{7,25},{8,22},{9,... | collective-permute-start | bytes 786440 | tf_op jit(solution)/shard_map/ppermute | solution.py:394
  243.1 48.4 %collective-permute-start.33 = (bf16[8,128,128]{2,1,0:T(8,128)(2,1)}, bf16[8,128,128]{2,1,0:T(8,128)(2,1)}, u32[]{:S(2)}, u32[]{:S(2)}) collective-permute-start(bf16[8,128,128]{2,1,0:T(8,128)(2,1)} %get-tuple-element.76), channel_id=1, source_target_pairs={{0,26},{1,27},{2,24},{3,25},{4,30},{5,31},{6,28},{7,29},{8,18},{9,... | collective-permute-start | bytes 786440 | tf_op jit(solution)/shard_map/ppermute | solution.py:394
  258.5 36.3 %collective-permute-start.34 = (bf16[8,128,128]{2,1,0:T(8,128)(2,1)}, bf16[8,128,128]{2,1,0:T(8,128)(2,1)}, u32[]{:S(2)}, u32[]{:S(2)}) collective-permute-start(bf16[8,128,128]{2,1,0:T(8,128)(2,1)} %get-tuple-element.77), channel_id=1, source_target_pairs={{0,25},{1,24},{2,27},{3,26},{4,29},{5,28},{6,31},{7,30},{8,17},{9,... | collective-permute-start | bytes 786440 | tf_op jit(solution)/shard_map/ppermute | solution.py:394
  263.9 44.5 %collective-permute-start.35 = (bf16[8,128,128]{2,1,0:T(8,128)(2,1)}, bf16[8,128,128]{2,1,0:T(8,128)(2,1)}, u32[]{:S(2)}, u32[]{:S(2)}) collective-permute-start(bf16[8,128,128]{2,1,0:T(8,128)(2,1)} %get-tuple-element.78), channel_id=1, source_target_pairs={{0,29},{1,28},{2,31},{3,30},{4,25},{5,24},{6,27},{7,26},{8,21},{9,... | collective-permute-start | bytes 786440 | tf_op jit(solution)/shard_map/ppermute | solution.py:394
  277.8 30.5 %collective-permute-start.36 = (bf16[8,128,128]{2,1,0:T(8,128)(2,1)}, bf16[8,128,128]{2,1,0:T(8,128)(2,1)}, u32[]{:S(2)}, u32[]{:S(2)}) collective-permute-start(bf16[8,128,128]{2,1,0:T(8,128)(2,1)} %get-tuple-element.79), channel_id=1, source_target_pairs={{0,31},{1,30},{2,29},{3,28},{4,27},{5,26},{6,25},{7,24},{8,23},{9,... | collective-permute-start | bytes 786440 | tf_op jit(solution)/shard_map/ppermute | solution.py:394
  277.9 30.6 %collective-permute-start.37 = (bf16[8,128,128]{2,1,0:T(8,128)(2,1)}, bf16[8,128,128]{2,1,0:T(8,128)(2,1)}, u32[]{:S(2)}, u32[]{:S(2)}) collective-permute-start(bf16[8,128,128]{2,1,0:T(8,128)(2,1)} %get-tuple-element.80), channel_id=1, source_target_pairs={{0,27},{1,26},{2,25},{3,24},{4,31},{5,30},{6,29},{7,28},{8,19},{9,... | collective-permute-start | bytes 786440 | tf_op jit(solution)/shard_map/ppermute | solution.py:394
  291.6 18.4 %collective-permute-start.44 = (f32[8,128]{1,0:T(8,128)}, f32[8,128]{1,0:T(8,128)S(1)}, u32[]{:S(2)}, u32[]{:S(2)}) collective-permute-start(f32[8,128]{1,0:T(8,128)} %get-tuple-element.81.refs_1_), channel_id=1, source_target_pairs={{0,7},{1,6},{2,5},{3,4},{4,3},{5,2},{6,1},{7,0},{8,15},{9,14},{10,... | collective-permute-start | bytes 12296 | tf_op jit(solution)/shard_map/ppermute | solution.py:351
  294.8 19.4 %collective-permute-start.43 = (f32[8,128]{1,0:T(8,128)}, f32[8,128]{1,0:T(8,128)S(1)}, u32[]{:S(2)}, u32[]{:S(2)}) collective-permute-start(f32[8,128]{1,0:T(8,128)} %get-tuple-element.81.refs_1_), channel_id=1, source_target_pairs={{0,6},{1,7},{2,4},{3,5},{4,2},{5,3},{6,0},{7,1},{8,14},{9,15},{10,... | collective-permute-start | bytes 12296 | tf_op jit(solution)/shard_map/ppermute | solution.py:351
  308.4 12.1 %collective-permute-start.42 = (f32[8,128]{1,0:T(8,128)}, f32[8,128]{1,0:T(8,128)S(1)}, u32[]{:S(2)}, u32[]{:S(2)}) collective-permute-start(f32[8,128]{1,0:T(8,128)} %get-tuple-element.81.refs_1_), channel_id=1, source_target_pairs={{0,5},{1,4},{2,7},{3,6},{4,1},{5,0},{6,3},{7,2},{8,13},{9,12},{10,... | collective-permute-start | bytes 12296 | tf_op jit(solution)/shard_map/ppermute | solution.py:351
  308.4 12.1 %collective-permute-start.41 = (f32[8,128]{1,0:T(8,128)}, f32[8,128]{1,0:T(8,128)S(1)}, u32[]{:S(2)}, u32[]{:S(2)}) collective-permute-start(f32[8,128]{1,0:T(8,128)} %get-tuple-element.81.refs_1_), channel_id=1, source_target_pairs={{0,4},{1,5},{2,6},{3,7},{4,0},{5,1},{6,2},{7,3},{8,12},{9,13},{10,... | collective-permute-start | bytes 12296 | tf_op jit(solution)/shard_map/ppermute | solution.py:351
  308.5 12.0 %collective-permute-start.40 = (f32[8,128]{1,0:T(8,128)}, f32[8,128]{1,0:T(8,128)S(1)}, u32[]{:S(2)}, u32[]{:S(2)}) collective-permute-start(f32[8,128]{1,0:T(8,128)} %get-tuple-element.81.refs_1_), channel_id=1, source_target_pairs={{0,3},{1,2},{2,1},{3,0},{4,7},{5,6},{6,5},{7,4},{8,11},{9,10},{10,... | collective-permute-start | bytes 12296 | tf_op jit(solution)/shard_map/ppermute | solution.py:351
  310.0 10.5 %collective-permute-start.39 = (f32[8,128]{1,0:T(8,128)}, f32[8,128]{1,0:T(8,128)S(1)}, u32[]{:S(2)}, u32[]{:S(2)}) collective-permute-start(f32[8,128]{1,0:T(8,128)} %get-tuple-element.81.refs_1_), channel_id=1, source_target_pairs={{0,2},{1,3},{2,0},{3,1},{4,6},{5,7},{6,4},{7,5},{8,10},{9,11},{10,... | collective-permute-start | bytes 12296 | tf_op jit(solution)/shard_map/ppermute | solution.py:351
  314.2 6.3 %collective-permute-start.38 = (f32[8,128]{1,0:T(8,128)}, f32[8,128]{1,0:T(8,128)S(1)}, u32[]{:S(2)}, u32[]{:S(2)}) collective-permute-start(f32[8,128]{1,0:T(8,128)} %get-tuple-element.81.refs_1_), channel_id=1, source_target_pairs={{0,1},{1,0},{2,3},{3,2},{4,5},{5,4},{6,7},{7,6},{8,9},{9,8},{10,11... | collective-permute-start | bytes 12296 | tf_op jit(solution)/shard_map/ppermute | solution.py:351
  (38 other events, 2172.1 us)
where the time goes:
time: 329 us; the launch traced here: 327 us
  starting transfers between devices  176 us (53%)
  Pallas kernels  98.9 us (30%)
  waiting for transfers between devices  35.1 us (11%)
  local copies, waits for them, and re-layouts  9.34 us (3%)
  other arithmetic  4.44 us (1%)
    ppermute x31, starting transfers between devices, per_device(): arrivals.append(lax.ppermute(part, AXES, pairs))  140 us
    pallas_call x5, Pallas kernels, project(): pl.pallas_call(kernel, out_shape=tuple(shapes) + (jax.ShapeDtypeStruct((8...  79.1 us
    ppermute x31, waiting for transfers between devices, per_device(): arrivals.append(lax.ppermute(part, AXES, pairs))  33.2 us
    ppermute x10, starting transfers between devices, spread(): lax.ppermute(value, axis, [(i, i ^ offset) for i in range(count)])  24.5 us
    pallas_call x9, Pallas kernels, place(): pl.pallas_call(functools.partial(place_kernel, layout=layout, first=first...  19.8 us
  transfers between devices with their start and end apart: 45, of which 9 were waited for; matrix products, arithmetic and copies ran while one was open for 3% of the time, Pallas kernels for 27%

commit v1 on v0

--- a/solution.py
+++ b/solution.py
@@ -14,7 +14,9 @@
 PAD = BS + 2 * RADIUS
 WIDE = 3 * BS
 BUFFERS = 4
-GROUPS = (2, 4, 8, 8, 10)
+ROW_SUM = 3
+LEAD = 3
+GROUPS = (1, 2, 4, 8, 8, 9)
 
 SHARPNESS = 32.0
 THRESHOLD = 0.5
@@ -55,19 +57,19 @@
 
 
 def exchange_order(row_count, col_count):
-    device_count = row_count * col_count
     quarter = max(1, col_count // 4)
-    long_part = [2, 3, 1] if col_count >= 4 else [1]
     rest = [r * col_count + c for r in range(row_count) for c in range(quarter)]
-    far = [long * quarter + other for other in rest for long in long_part]
-    near = [other for other in rest if other]
-    order = []
-    while far or near:
-        order, far = order + far[:3], far[3:]
-        if near:
-            order.append(near.pop(0))
-    order = [d for d in order if 0 < d < device_count]
-    assert sorted(order) == list(range(1, device_count))
+    middle = [part * quarter + other for other in rest for part in (2, 3)]
+    light = []
+    for other in rest:
+        light += [quarter + other, other]
+    light.reverse()
+    order, middle = middle[:LEAD], middle[LEAD:]
+    while middle or light:
+        order += light[:2] + middle[:2]
+        light, middle = light[2:], middle[2:]
+    order = [d for d in order if d]
+    assert sorted(order) == list(range(1, row_count * col_count))
     return order
 
 
@@ -303,7 +305,7 @@
     return results[:-1], results[-1]
 
 
-def place_kernel(meta_ref, out_in, *refs, layout, first, count, parts):
+def place_kernel(meta_ref, out_in, *refs, layout, first, count, parts, finish):
     del out_in
     arrived, refs = refs[:count], refs[count:]
     addends, refs = refs[:parts], refs[parts:]
@@ -314,19 +316,21 @@
             slot = meta_ref[layout.place + (first + g) * capacity + r]
             pltpu.make_async_copy(arrived[g].at[r], out.at[slot], sem).start()
     if parts:
-        refs[1][...] = pairwise_sum([addend[...] for addend in addends])
+        total = pairwise_sum([addend[...] for addend in addends])
+        refs[1][...] = finish(total) if finish else total
     everything = out.at[pl.ds(0, count * capacity)]
     pltpu.make_async_copy(everything, everything, sem).wait()
 
 
-def place(meta, out, arrived, addends, *, layout, first):
+def place(meta, out, arrived, addends, *, layout, first, finish=None):
     anywhere = pl.BlockSpec(memory_space=pl.ANY)
     vmem = pl.BlockSpec(memory_space=pltpu.VMEM)
     shapes = [jax.ShapeDtypeStruct(out.shape, out.dtype)]
-    shapes += [jax.ShapeDtypeStruct(a.shape, a.dtype) for a in addends[:1]]
+    shapes += [jax.ShapeDtypeStruct((1, 1) if finish else a.shape, a.dtype)
+               for a in addends[:1]]
     results = pl.pallas_call(
         functools.partial(place_kernel, layout=layout, first=first, count=len(arrived),
-                          parts=len(addends)),
+                          parts=len(addends), finish=finish),
         out_shape=tuple(shapes),
         in_specs=[pl.BlockSpec(memory_space=pltpu.SMEM), anywhere]
         + [vmem] * (len(arrived) + len(addends)),
@@ -348,7 +352,8 @@
     count = lax.axis_size(axis)
     parts = [value]
     for offset in range(1, count):
-        parts.append(lax.ppermute(value, axis, [(i, i ^ offset) for i in range(count)]))
+        part = lax.ppermute(value, axis, [(i, i ^ offset) for i in range(count)])
+        parts.append(pltpu.with_memory_space_constraint(part, pltpu.VMEM))
     return parts
 
 
@@ -391,7 +396,8 @@
         for offset, part in zip(group, sent):
             if offset:
                 pairs = [(i, i ^ offset) for i in range(device_count)]
-                arrivals.append(lax.ppermute(part, AXES, pairs))
+                part = lax.ppermute(part, AXES, pairs)
+                arrivals.append(pltpu.with_memory_space_constraint(part, pltpu.VMEM))
             else:
                 out = part
         first += len(group)
@@ -400,18 +406,23 @@
     bulk = len(arrivals) - sum(tail)
     sizes = [bulk % (4 * unit)] + [4 * unit] * (bulk // (4 * unit)) + tail
     sizes = [size for size in sizes if size]
+    grid_cells = float(tile_rows * tile_cols * device_count)
+
+    def constraint_of(total):
+        volume = jnp.sum(jnp.sum(total, axis=0, keepdims=True), axis=1, keepdims=True)
+        return volume / grid_cells / VOLUME_TARGET - 1.0
+
     begin = 0
     addends = spread(acc, "row")
     for index, size in enumerate(sizes):
-        now = addends if index in (len(sizes) // 2, len(sizes) - 1) else []
-        out, total = place(meta, out, arrivals[begin:begin + size], now,
-                           layout=layout, first=begin)
-        if index == len(sizes) // 2:
+        last = index == len(sizes) - 1
+        out, total = place(meta, out, arrivals[begin:begin + size],
+                           addends if last or index == ROW_SUM else [],
+                           layout=layout, first=begin, finish=constraint_of if last else None)
+        if index == ROW_SUM:
             addends = spread(total, "col")
         begin += size
-    grid_cells = float(tile_rows * tile_cols * device_count)
-    constraint = jnp.sum(total) / grid_cells / VOLUME_TARGET - 1.0
-    return out, constraint
+    return out, total.reshape(())
 
 
 def solution(mesh):

time: 329 us -> 313 us (0.951)
  starting transfers between devices: 176 us -> 94.2 us
  waiting for transfers between devices: 35.1 us -> 94.5 us
  local copies, waits for them, and re-layouts: 9.34 us -> 18.2 us
    ppermute x41, starting transfers between devices: 165 us -> 83.1 us  [the longest x31 69 us: per_device(): part = lax.ppermute(part, AXES, pairs)]
    ppermute x41, waiting for transfers between devices: 33.4 us -> 92.7 us  [the longest x31 92.6 us: per_device(): part = lax.ppermute(part, AXES, pairs)]
    unnamed x85 -> x79, local copies, waits for them, and re-layouts: 1.64 us -> 10.6 us
    pallas_call x5 -> x6, Pallas kernels: 79.1 us -> 82.5 us  [project(): pl.pallas_call(kernel, out_shape=tuple(shapes) + (jax.ShapeDtypeStruct((8...]
  transfers between devices with their start and end apart: 45 -> 45, of which waited for: 9 -> 13; matrix products, arithmetic and copies ran while one was open for 3% -> 3% of each run, Pallas kernels for 27% -> 30%
where the time goes in v1:
time: 313 us; the launch traced here: 311 us
  Pallas kernels  99.7 us (32%)
  waiting for transfers between devices  94.5 us (30%)
  starting transfers between devices  94.2 us (30%)
  local copies, waits for them, and re-layouts  18.2 us (6%)
  other arithmetic  3.15 us (1%)
    ppermute x31, waiting for transfers between devices, per_device(): part = lax.ppermute(part, AXES, pairs)  92.6 us
    pallas_call x6, Pallas kernels, project(): pl.pallas_call(kernel, out_shape=tuple(shapes) + (jax.ShapeDtypeStruct((8...  82.5 us
    ppermute x31, starting transfers between devices, per_device(): part = lax.ppermute(part, AXES, pairs)  69 us
    pallas_call x9, Pallas kernels, place(): pl.pallas_call(functools.partial(place_kernel, layout=layout, first=first...  17.2 us
    ppermute x10, starting transfers between devices, spread(): part = lax.ppermute(value, axis, [(i, i ^ offset) for i in range(count)])  14.1 us
    unnamed x79, local copies, waits for them, and re-layouts  10.6 us
  transfers between devices with their start and end apart: 45, of which 13 were waited for; matrix products, arithmetic and copies ran while one was open for 3% of the time, Pallas kernels for 30%

profile of v1, /device:TPU:0, one launch (start us, length us, event | category | flops | bytes accessed | tf_op | source)
XLA Modules:
  0.0 311.4 jit_solution(6834202850413105679)
XLA Ops:
  3.0 3.0 collective-permute-start
  14.9 5.5 %collective-permute-start.2 = (f32[16,1056]{1,0:T(8,128)S(1)}, f32[16,1056]{1,0:T(8,128)S(1)}, u32[]{:S(2)}, u32[]{:S(2)}) collective-permute-start(f32[16,1056]{1,0:T(8,128)S(1)} %concatenate.18), channel_id=1, source_target_pairs={{0,1},{1,2},{2,3},{3,4},{4,5},{5,6},{6,7},{8,9},{9,10},{10,11},{11... | collective-permute-start | bytes 202760 | tf_op jit(solution)/shard_map/ppermute | solution.py:92
  21.7 1.5 collective-permute-done.2
  25.1 5.3 %project.6 = (bf16[8,128,128]{2,1,0:T(8,128)(2,1)}, f32[8,128]{1,0:T(8,128)}) custom-call(s32[768]{0:T(1024)} %copy-done.30, f32[1024,4096]{1,0:T(8,128)} %dens.11, f32[16,4096]{1,0:T(8,128)} %copy-done.29, f32[16,4096]{1,0:T(8,128)} %copy-done.28, f32[1056,128]{1,0:T(8,128)} %pad_bitcast_fusion.1.left, f32[1056,128]{1,0:T(8,128)} %pad_bitcast_fusion.right, ...), custom_call_target="tpu_custom_call" | custom-call | flops 2400000000 | bytes 2400000 | tf_op jit(solution)/shard_map/project/pallas_call | solution.py:289
  30.4 5.7 %collective-permute-start.4 = (bf16[8,128,128]{2,1,0:T(8,128)(2,1)}, bf16[8,128,128]{2,1,0:T(8,128)(2,1)S(1)}, u32[]{:S(2)}, u32[]{:S(2)}) collective-permute-start(bf16[8,128,128]{2,1,0:T(8,128)(2,1)} %get-tuple-element.50), channel_id=1, source_target_pairs={{0,4},{1,5},{2,6},{3,7},{4,0},{5,1},{6,2},{7,3},{8,12},{9,13},{10,... | collective-permute-start | bytes 786440 | tf_op jit(solution)/shard_map/ppermute | solution.py:399
  36.1 7.2 %project.7 = (bf16[8,128,128]{2,1,0:T(8,128)(2,1)}, bf16[8,128,128]{2,1,0:T(8,128)(2,1)}, f32[8,128]{1,0:T(8,128)}) custom-call(s32[768]{0:T(1024)} %copy-done.30, f32[1024,4096]{1,0:T(8,128)} %dens.11, f32[16,4096]{1,0:T(8,128)} %copy-done.29, f32[16,4096]{1,0:T(8,128)} %copy-done.28, f32[1056,128]{1,0:T(8,128)} %pad_bitcast_fusion.1.left, ...), custom_call_target="tpu_custom_call" | custom-call | flops 4800000000 | bytes 4800000 | tf_op jit(solution)/shard_map/project/pallas_call | solution.py:289
  43.3 11.2 %project.8 = (bf16[8,128,128]{2,1,0:T(8,128)(2,1)}, bf16[8,128,128]{2,1,0:T(8,128)(2,1)}, bf16[8,128,128]{2,1,0:T(8,128)(2,1)}, bf16[8,128,128]{2,1,0:T(8,128)(2,1)}, f32[8,128]{1,0:T(8,128)}) custom-call(s32[768]{0:T(1024)} %copy-done.30, f32[1024,4096]{1,0:T(8,128)} %dens.11, f32[16,4096]{1,0:T(8,128)} %copy-done.29, f32[16,4096]{1,0:T(8,128)} %copy-done.28, ...), custom_call_target="tpu_custom_call" | custom-call | flops 9600000000 | bytes 9600000 | tf_op jit(solution)/shard_map/project/pallas_call | solution.py:289
  54.5 19.0 %project.9 = (bf16[8,128,128]{2,1,0:T(8,128)(2,1)}, bf16[8,128,128]{2,1,0:T(8,128)(2,1)}, bf16[8,128,128]{2,1,0:T(8,128)(2,1)}, bf16[8,128,128]{2,1,0:T(8,128)(2...) custom-call(s32[768]{0:T(1024)} %copy-done.30, ...), custom_call_target="tpu_custom_call" | custom-call | flops 19200000000 | bytes 19200000 | tf_op jit(solution)/shard_map/project/pallas_call | solution.py:289
  73.5 18.9 %project.10 = (bf16[8,128,128]{2,1,0:T(8,128)(2,1)}, bf16[8,128,128]{2,1,0:T(8,128)(2,1)}, bf16[8,128,128]{2,1,0:T(8,128)(2,1)}, bf16[8,128,128]{2,1,0:T(8,128)(...) custom-call(s32[768]{0:T(1024)} %copy-done.30, ...), custom_call_target="tpu_custom_call" | custom-call | flops 19200000000 | bytes 19200000 | tf_op jit(solution)/shard_map/project/pallas_call | solution.py:289
  92.5 20.9 %project.11 = (bf16[8,128,128]{2,1,0:T(8,128)(2,1)}, bf16[8,128,128]{2,1,0:T(8,128)(2,1)}, bf16[8,128,128]{2,1,0:T(8,128)(2,1)}, bf16[8,128,128]{2,1,0:T(8,128)(...) custom-call(s32[768]{0:T(1024)} %copy-done.30, ...), custom_call_target="tpu_custom_call" | custom-call | flops 21600000000 | bytes 21600000 | tf_op jit(solution)/shard_map/project/pallas_call | solution.py:289
  117.5 1.6 collective-permute-start.7
  119.2 1.8 collective-permute-start.8
  121.0 3.1 collective-permute-start.9
  124.1 2.3 collective-permute-done.5.refs_1_
  126.5 8.6 %collective-permute-start.10 = (bf16[8,128,128]{2,1,0:T(8,128)(2,1)}, bf16[8,128,128]{2,1,0:T(8,128)(2,1)S(1)}, u32[]{:S(2)}, u32[]{:S(2)}) collective-permute-start(bf16[8,128,128]{2,1,0:T(8,128)(2,1)} %get-tuple-element.56), channel_id=1, source_target_pairs={{0,12},{1,13},{2,14},{3,15},{4,8},{5,9},{6,10},{7,11},{8,4},{9,5},... | collective-permute-start | bytes 786440 | tf_op jit(solution)/shard_map/ppermute | solution.py:399
  135.1 17.7 %collective-permute-done.6.refs_2_ = bf16[8,128,128]{2,1,0:T(8,128)(2,1)S(1)} collective-permute-done((bf16[8,128,128]{2,1,0:T(8,128)(2,1)S(1)}, bf16[8,128,128]{2,1,0:T(8,128)(2,1)S(1)}, u32[]{:S(2)}, u32[]{:S(2)}) %collective-permute-start.6) | collective-permute-done | bytes 262176 | tf_op jit(solution)/shard_map/ppermute | solution.py:399
  152.8 1.6 collective-permute-start.13
  154.5 4.4 %collective-permute-start.14 = (bf16[8,128,128]{2,1,0:T(8,128)(2,1)}, bf16[8,128,128]{2,1,0:T(8,128)(2,1)S(1)}, u32[]{:S(2)}, u32[]{:S(2)}) collective-permute-start(bf16[8,128,128]{2,1,0:T(8,128)(2,1)} %get-tuple-element.60), channel_id=1, source_target_pairs={{0,13},{1,12},{2,15},{3,14},{4,9},{5,8},{6,11},{7,10},{8,5},{9,4},... | collective-permute-start | bytes 786440 | tf_op jit(solution)/shard_map/ppermute | solution.py:399
  158.9 15.3 %collective-permute-done.10.refs_2_ = bf16[8,128,128]{2,1,0:T(8,128)(2,1)S(1)} collective-permute-done((bf16[8,128,128]{2,1,0:T(8,128)(2,1)}, bf16[8,128,128]{2,1,0:T(8,128)(2,1)S(1)}, u32[]{:S(2)}, u32[]{:S(2)}) %collective-permute-start.10) | collective-permute-done | bytes 262176 | tf_op jit(solution)/shard_map/ppermute | solution.py:399
  174.2 2.5 collective-permute-start.16
  178.0 3.4 %collective-permute-start.18 = (bf16[8,128,128]{2,1,0:T(8,128)(2,1)}, bf16[8,128,128]{2,1,0:T(8,128)(2,1)S(1)}, u32[]{:S(2)}, u32[]{:S(2)}) collective-permute-start(bf16[8,128,128]{2,1,0:T(8,128)(2,1)} %get-tuple-element.64), channel_id=1, source_target_pairs={{0,20},{1,21},{2,22},{3,23},{4,16},{5,17},{6,18},{7,19},{8,28},{9,... | collective-permute-start | bytes 786440 | tf_op jit(solution)/shard_map/ppermute | solution.py:399
  181.4 4.4 %collective-permute-done.14.refs_2_ = bf16[8,128,128]{2,1,0:T(8,128)(2,1)S(1)} collective-permute-done((bf16[8,128,128]{2,1,0:T(8,128)(2,1)}, bf16[8,128,128]{2,1,0:T(8,128)(2,1)S(1)}, u32[]{:S(2)}, u32[]{:S(2)}) %collective-permute-start.14) | collective-permute-done | bytes 262176 | tf_op jit(solution)/shard_map/ppermute | solution.py:399
  186.7 13.7 %collective-permute-done.15.refs_3_ = bf16[8,128,128]{2,1,0:T(8,128)(2,1)S(1)} collective-permute-done((bf16[8,128,128]{2,1,0:T(8,128)(2,1)S(1)}, bf16[8,128,128]{2,1,0:T(8,128)(2,1)S(1)}, u32[]{:S(2)}, u32[]{:S(2)}) %collective-permute-start.15) | collective-permute-done | bytes 262176 | tf_op jit(solution)/shard_map/ppermute | solution.py:399
  201.8 2.3 collective-permute-start.24
  206.3 4.1 %collective-permute-done.18.refs_2_ = bf16[8,128,128]{2,1,0:T(8,128)(2,1)S(1)} collective-permute-done((bf16[8,128,128]{2,1,0:T(8,128)(2,1)}, bf16[8,128,128]{2,1,0:T(8,128)(2,1)S(1)}, u32[]{:S(2)}, u32[]{:S(2)}) %collective-permute-start.18) | collective-permute-done | bytes 262176 | tf_op jit(solution)/shard_map/ppermute | solution.py:399
  211.9 8.6 %collective-permute-done.23.refs_0_ = bf16[8,128,128]{2,1,0:T(8,128)(2,1)S(1)} collective-permute-done((bf16[8,128,128]{2,1,0:T(8,128)(2,1)}, bf16[8,128,128]{2,1,0:T(8,128)(2,1)S(1)}, u32[]{:S(2)}, u32[]{:S(2)}) %collective-permute-start.23) | collective-permute-done | bytes 262176 | tf_op jit(solution)/shard_map/ppermute | solution.py:399
  220.5 6.5 %collective-permute-start.28 = (bf16[8,128,128]{2,1,0:T(8,128)(2,1)}, bf16[8,128,128]{2,1,0:T(8,128)(2,1)S(1)}, u32[]{:S(2)}, u32[]{:S(2)}) collective-permute-start(bf16[8,128,128]{2,1,0:T(8,128)(2,1)} %get-tuple-element.73), channel_id=1, source_target_pairs={{0,23},{1,22},{2,21},{3,20},{4,19},{5,18},{6,17},{7,16},{8,31},{9,... | collective-permute-start | bytes 786440 | tf_op jit(solution)/shard_map/ppermute | solution.py:399
  227.4 5.8 %collective-permute-done.25.refs_2_ = bf16[8,128,128]{2,1,0:T(8,128)(2,1)S(1)} collective-permute-done((bf16[8,128,128]{2,1,0:T(8,128)(2,1)}, bf16[8,128,128]{2,1,0:T(8,128)(2,1)S(1)}, u32[]{:S(2)}, u32[]{:S(2)}) %collective-permute-start.25) | collective-permute-done | bytes 262176 | tf_op jit(solution)/shard_map/ppermute | solution.py:399
  233.9 9.3 %collective-permute-start.31 = (bf16[8,128,128]{2,1,0:T(8,128)(2,1)}, bf16[8,128,128]{2,1,0:T(8,128)(2,1)S(1)}, u32[]{:S(2)}, u32[]{:S(2)}) collective-permute-start(bf16[8,128,128]{2,1,0:T(8,128)(2,1)} %get-tuple-element.76), channel_id=1, source_target_pairs={{0,10},{1,11},{2,8},{3,9},{4,14},{5,15},{6,12},{7,13},{8,2},{9,3},... | collective-permute-start | bytes 786440 | tf_op jit(solution)/shard_map/ppermute | solution.py:399
  243.9 2.1 collective-permute-start.32
  246.8 5.3 %collective-permute-start.33 = (bf16[8,128,128]{2,1,0:T(8,128)(2,1)}, bf16[8,128,128]{2,1,0:T(8,128)(2,1)}, u32[]{:S(2)}, u32[]{:S(2)}) collective-permute-start(bf16[8,128,128]{2,1,0:T(8,128)(2,1)} %get-tuple-element.78), channel_id=1, source_target_pairs={{0,29},{1,28},{2,31},{3,30},{4,25},{5,24},{6,27},{7,26},{8,21},{9,... | collective-permute-start | bytes 786440 | tf_op jit(solution)/shard_map/ppermute | solution.py:399
  252.0 13.8 %collective-permute-done.29.refs_2_ = bf16[8,128,128]{2,1,0:T(8,128)(2,1)S(1)} collective-permute-done((bf16[8,128,128]{2,1,0:T(8,128)(2,1)}, bf16[8,128,128]{2,1,0:T(8,128)(2,1)S(1)}, u32[]{:S(2)}, u32[]{:S(2)}) %collective-permute-start.29) | collective-permute-done | bytes 262176 | tf_op jit(solution)/shard_map/ppermute | solution.py:399
  267.3 1.9 collective-permute-start.35
  269.9 2.8 collective-permute-start.36
  273.9 1.7 place.9.out_in
  275.6 1.8 place.10.out_in
  278.4 1.8 place.11.out_in
  280.2 2.4 place.12
  282.6 3.2 %collective-permute-start.44 = (f32[8,128]{1,0:T(8,128)}, f32[8,128]{1,0:T(8,128)S(1)}, u32[]{:S(2)}, u32[]{:S(2)}) collective-permute-start(f32[8,128]{1,0:T(8,128)} %get-tuple-element.83.refs_1_), channel_id=1, source_target_pairs={{0,7},{1,6},{2,5},{3,4},{4,3},{5,2},{6,1},{7,0},{8,15},{9,14},{10,... | collective-permute-start | bytes 12296 | tf_op jit(solution)/shard_map/ppermute | solution.py:355
  285.8 6.7 %collective-permute-done.34.refs_3_ = bf16[8,128,128]{2,1,0:T(8,128)(2,1)} collective-permute-done((bf16[8,128,128]{2,1,0:T(8,128)(2,1)}, bf16[8,128,128]{2,1,0:T(8,128)(2,1)}, u32[]{:S(2)}, u32[]{:S(2)}) %collective-permute-start.34) | collective-permute-done | bytes 262176 | tf_op jit(solution)/shard_map/ppermute | solution.py:399
  292.5 3.1 collective-permute-start.43
  295.6 2.0 collective-permute-start.41
  297.9 3.6 %collective-permute-start.39 = (f32[8,128]{1,0:T(8,128)}, f32[8,128]{1,0:T(8,128)S(1)}, u32[]{:S(2)}, u32[]{:S(2)}) collective-permute-start(f32[8,128]{1,0:T(8,128)} %get-tuple-element.83.refs_1_), channel_id=1, source_target_pairs={{0,2},{1,3},{2,0},{3,1},{4,6},{5,7},{6,4},{7,5},{8,10},{9,11},{10,... | collective-permute-start | bytes 12296 | tf_op jit(solution)/shard_map/ppermute | solution.py:355
  301.5 1.8 place.13.out_in
  303.4 1.8 place.14.out_in
  305.2 2.0 place.15.out_in
  307.2 1.8 place.16.out_in
  309.1 2.2 place.17
  (168 shorter events, 32.9 us)
Async XLA Ops:
  1.7 11.2 %collective-permute-start.1 = (f32[16,4096]{1,0:T(8,128)S(1)}, f32[16,4096]{1,0:T(8,128)S(1)}, u32[]{:S(2)}, u32[]{:S(2)}) collective-permute-start(f32[16,4096]{1,0:T(8,128)S(1)} %get-tuple-element.90), channel_id=1, source_target_pairs={{8,0},{16,8},{24,16},{9,1},{17,9},{25,17},{10,2},{18,10},{26,18},{... | collective-permute-start | bytes 786440 | tf_op jit(solution)/shard_map/ppermute | solution.py:85
  3.0 10.1 %collective-permute-start = (f32[16,4096]{1,0:T(8,128)S(1)}, f32[16,4096]{1,0:T(8,128)S(1)}, u32[]{:S(2)}, u32[]{:S(2)}) collective-permute-start(f32[16,4096]{1,0:T(8,128)S(1)} %get-tuple-element.91), channel_id=1, source_target_pairs={{0,8},{8,16},{16,24},{1,9},{9,17},{17,25},{2,10},{10,18},{18,26},{... | collective-permute-start | bytes 786440 | tf_op jit(solution)/shard_map/ppermute | solution.py:84
  13.3 7.3 %collective-permute-start.3 = (f32[16,1056]{1,0:T(8,128)S(1)}, f32[16,1056]{1,0:T(8,128)S(1)}, u32[]{:S(2)}, u32[]{:S(2)}) collective-permute-start(f32[16,1056]{1,0:T(8,128)S(1)} %concatenate.19), channel_id=1, source_target_pairs={{1,0},{2,1},{3,2},{4,3},{5,4},{6,5},{7,6},{9,8},{10,9},{11,10},{12... | collective-permute-start | bytes 202760 | tf_op jit(solution)/shard_map/ppermute | solution.py:93
  14.9 8.3 %collective-permute-start.2 = (f32[16,1056]{1,0:T(8,128)S(1)}, f32[16,1056]{1,0:T(8,128)S(1)}, u32[]{:S(2)}, u32[]{:S(2)}) collective-permute-start(f32[16,1056]{1,0:T(8,128)S(1)} %concatenate.18), channel_id=1, source_target_pairs={{0,1},{1,2},{2,3},{3,4},{4,5},{5,6},{6,7},{8,9},{9,10},{10,11},{11... | collective-permute-start | bytes 202760 | tf_op jit(solution)/shard_map/ppermute | solution.py:92
  30.4 90.7 %collective-permute-start.4 = (bf16[8,128,128]{2,1,0:T(8,128)(2,1)}, bf16[8,128,128]{2,1,0:T(8,128)(2,1)S(1)}, u32[]{:S(2)}, u32[]{:S(2)}) collective-permute-start(bf16[8,128,128]{2,1,0:T(8,128)(2,1)} %get-tuple-element.50), channel_id=1, source_target_pairs={{0,4},{1,5},{2,6},{3,7},{4,0},{5,1},{6,2},{7,3},{8,12},{9,13},{10,... | collective-permute-start | bytes 786440 | tf_op jit(solution)/shard_map/ppermute | solution.py:399
  92.5 81.7 %copy-start.32 = (bf16[8,128,128]{2,1,0:T(8,128)(2,1)S(1)}, bf16[8,128,128]{2,1,0:T(8,128)(2,1)}, u32[]{:S(2)}) copy-start(bf16[8,128,128]{2,1,0:T(8,128)(2,1)} %get-tuple-element.62) | copy-start | bytes 786436
  92.5 84.2 %copy-start.31 = (bf16[8,128,128]{2,1,0:T(8,128)(2,1)S(1)}, bf16[8,128,128]{2,1,0:T(8,128)(2,1)}, u32[]{:S(2)}) copy-start(bf16[8,128,128]{2,1,0:T(8,128)(2,1)} %get-tuple-element.63) | copy-start | bytes 786436
  113.4 3.3 %collective-permute-start.22 = (f32[8,128]{1,0:T(8,128)}, f32[8,128]{1,0:T(8,128)S(1)}, u32[]{:S(2)}, u32[]{:S(2)}) collective-permute-start(f32[8,128]{1,0:T(8,128)} %get-tuple-element.66.refs_4_), channel_id=1, source_target_pairs={{0,24},{8,16},{16,8},{24,0},{1,25},{9,17},{17,9},{25,1},{2,26},{10... | collective-permute-start | bytes 12296 | tf_op jit(solution)/shard_map/ppermute | solution.py:355
  113.5 4.1 %collective-permute-start.21 = (f32[8,128]{1,0:T(8,128)}, f32[8,128]{1,0:T(8,128)S(1)}, u32[]{:S(2)}, u32[]{:S(2)}) collective-permute-start(f32[8,128]{1,0:T(8,128)} %get-tuple-element.66.refs_4_), channel_id=1, source_target_pairs={{0,16},{8,24},{16,0},{24,8},{1,17},{9,25},{17,1},{25,9},{2,18},{10... | collective-permute-start | bytes 12296 | tf_op jit(solution)/shard_map/ppermute | solution.py:355
  114.8 4.3 %collective-permute-start.20 = (f32[8,128]{1,0:T(8,128)}, f32[8,128]{1,0:T(8,128)S(1)}, u32[]{:S(2)}, u32[]{:S(2)}) collective-permute-start(f32[8,128]{1,0:T(8,128)} %get-tuple-element.66.refs_4_), channel_id=1, source_target_pairs={{0,8},{8,0},{16,24},{24,16},{1,9},{9,1},{17,25},{25,17},{2,10},{10... | collective-permute-start | bytes 12296 | tf_op jit(solution)/shard_map/ppermute | solution.py:355
  115.3 11.1 %collective-permute-start.5 = (bf16[8,128,128]{2,1,0:T(8,128)(2,1)S(1)}, bf16[8,128,128]{2,1,0:T(8,128)(2,1)S(1)}, u32[]{:S(2)}, u32[]{:S(2)}) collective-permute-start(bf16[8,128,128]{2,1,0:T(8,128)(2,1)S(1)} %copy-done.37), channel_id=1, source_target_pairs={{0,6},{1,7},{2,4},{3,5},{4,2},{5,3},{6,0},{7,1},{8,14},{9,15},{10,... | collective-permute-start | bytes 786440 | tf_op jit(solution)/shard_map/ppermute | solution.py:399
  116.7 36.0 %collective-permute-start.6 = (bf16[8,128,128]{2,1,0:T(8,128)(2,1)S(1)}, bf16[8,128,128]{2,1,0:T(8,128)(2,1)S(1)}, u32[]{:S(2)}, u32[]{:S(2)}) collective-permute-start(bf16[8,128,128]{2,1,0:T(8,128)(2,1)S(1)} %copy-done.36), channel_id=1, source_target_pairs={{0,5},{1,4},{2,7},{3,6},{4,1},{5,0},{6,3},{7,2},{8,13},{9,12},{10,... | collective-permute-start | bytes 786440 | tf_op jit(solution)/shard_map/ppermute | solution.py:399
  117.5 35.2 %collective-permute-start.7 = (bf16[8,128,128]{2,1,0:T(8,128)(2,1)S(1)}, bf16[8,128,128]{2,1,0:T(8,128)(2,1)S(1)}, u32[]{:S(2)}, u32[]{:S(2)}) collective-permute-start(bf16[8,128,128]{2,1,0:T(8,128)(2,1)S(1)} %copy-done.35), channel_id=1, source_target_pairs={{0,25},{1,24},{2,27},{3,26},{4,29},{5,28},{6,31},{7,30},{8,17},{9,... | collective-permute-start | bytes 786440 | tf_op jit(solution)/shard_map/ppermute | solution.py:399
  119.2 33.7 %collective-permute-start.8 = (bf16[8,128,128]{2,1,0:T(8,128)(2,1)S(1)}, bf16[8,128,128]{2,1,0:T(8,128)(2,1)S(1)}, u32[]{:S(2)}, u32[]{:S(2)}) collective-permute-start(bf16[8,128,128]{2,1,0:T(8,128)(2,1)S(1)} %copy-done.34), channel_id=1, source_target_pairs={{0,27},{1,26},{2,25},{3,24},{4,31},{5,30},{6,29},{7,28},{8,19},{9,... | collective-permute-start | bytes 786440 | tf_op jit(solution)/shard_map/ppermute | solution.py:399
  121.0 33.5 %collective-permute-start.9 = (bf16[8,128,128]{2,1,0:T(8,128)(2,1)}, bf16[8,128,128]{2,1,0:T(8,128)(2,1)S(1)}, u32[]{:S(2)}, u32[]{:S(2)}) collective-permute-start(bf16[8,128,128]{2,1,0:T(8,128)(2,1)} %get-tuple-element.55), channel_id=1, source_target_pairs={{0,7},{1,6},{2,5},{3,4},{4,3},{5,2},{6,1},{7,0},{8,15},{9,14},{10,... | collective-permute-start | bytes 786440 | tf_op jit(solution)/shard_map/ppermute | solution.py:399
  126.5 47.7 %collective-permute-start.10 = (bf16[8,128,128]{2,1,0:T(8,128)(2,1)}, bf16[8,128,128]{2,1,0:T(8,128)(2,1)S(1)}, u32[]{:S(2)}, u32[]{:S(2)}) collective-permute-start(bf16[8,128,128]{2,1,0:T(8,128)(2,1)} %get-tuple-element.56), channel_id=1, source_target_pairs={{0,12},{1,13},{2,14},{3,15},{4,8},{5,9},{6,10},{7,11},{8,4},{9,5},... | collective-permute-start | bytes 786440 | tf_op jit(solution)/shard_map/ppermute | solution.py:399
  152.7 21.4 %collective-permute-start.11 = (bf16[8,128,128]{2,1,0:T(8,128)(2,1)}, bf16[8,128,128]{2,1,0:T(8,128)(2,1)S(1)}, u32[]{:S(2)}, u32[]{:S(2)}) collective-permute-start(bf16[8,128,128]{2,1,0:T(8,128)(2,1)} %get-tuple-element.57), channel_id=1, source_target_pairs={{0,24},{1,25},{2,26},{3,27},{4,28},{5,29},{6,30},{7,31},{8,16},{9,... | collective-permute-start | bytes 786440 | tf_op jit(solution)/shard_map/ppermute | solution.py:399
  152.7 23.9 %collective-permute-start.12 = (bf16[8,128,128]{2,1,0:T(8,128)(2,1)}, bf16[8,128,128]{2,1,0:T(8,128)(2,1)S(1)}, u32[]{:S(2)}, u32[]{:S(2)}) collective-permute-start(bf16[8,128,128]{2,1,0:T(8,128)(2,1)} %get-tuple-element.58), channel_id=1, source_target_pairs={{0,26},{1,27},{2,24},{3,25},{4,30},{5,31},{6,28},{7,29},{8,18},{9,... | collective-permute-start | bytes 786440 | tf_op jit(solution)/shard_map/ppermute | solution.py:399
  152.8 25.2 %collective-permute-start.13 = (bf16[8,128,128]{2,1,0:T(8,128)(2,1)}, bf16[8,128,128]{2,1,0:T(8,128)(2,1)S(1)}, u32[]{:S(2)}, u32[]{:S(2)}) collective-permute-start(bf16[8,128,128]{2,1,0:T(8,128)(2,1)} %get-tuple-element.59), channel_id=1, source_target_pairs={{0,14},{1,15},{2,12},{3,13},{4,10},{5,11},{6,8},{7,9},{8,6},{9,7},... | collective-permute-start | bytes 786440 | tf_op jit(solution)/shard_map/ppermute | solution.py:399
  154.5 31.3 %collective-permute-start.14 = (bf16[8,128,128]{2,1,0:T(8,128)(2,1)}, bf16[8,128,128]{2,1,0:T(8,128)(2,1)S(1)}, u32[]{:S(2)}, u32[]{:S(2)}) collective-permute-start(bf16[8,128,128]{2,1,0:T(8,128)(2,1)} %get-tuple-element.60), channel_id=1, source_target_pairs={{0,13},{1,12},{2,15},{3,14},{4,9},{5,8},{6,11},{7,10},{8,5},{9,4},... | collective-permute-start | bytes 786440 | tf_op jit(solution)/shard_map/ppermute | solution.py:399
  174.2 26.2 %collective-permute-start.15 = (bf16[8,128,128]{2,1,0:T(8,128)(2,1)S(1)}, bf16[8,128,128]{2,1,0:T(8,128)(2,1)S(1)}, u32[]{:S(2)}, u32[]{:S(2)}) collective-permute-start(bf16[8,128,128]{2,1,0:T(8,128)(2,1)S(1)} %copy-done.33), channel_id=1, source_target_pairs={{0,17},{1,16},{2,19},{3,18},{4,21},{5,20},{6,23},{7,22},{8,25},{9,... | collective-permute-start | bytes 786440 | tf_op jit(solution)/shard_map/ppermute | solution.py:399
  174.2 26.9 %collective-permute-start.16 = (bf16[8,128,128]{2,1,0:T(8,128)(2,1)S(1)}, bf16[8,128,128]{2,1,0:T(8,128)(2,1)S(1)}, u32[]{:S(2)}, u32[]{:S(2)}) collective-permute-start(bf16[8,128,128]{2,1,0:T(8,128)(2,1)S(1)} %copy-done.32), channel_id=1, source_target_pairs={{0,19},{1,18},{2,17},{3,16},{4,23},{5,22},{6,21},{7,20},{8,27},{9,... | collective-permute-start | bytes 786440 | tf_op jit(solution)/shard_map/ppermute | solution.py:399
  176.7 27.4 %collective-permute-start.17 = (bf16[8,128,128]{2,1,0:T(8,128)(2,1)S(1)}, bf16[8,128,128]{2,1,0:T(8,128)(2,1)S(1)}, u32[]{:S(2)}, u32[]{:S(2)}) collective-permute-start(bf16[8,128,128]{2,1,0:T(8,128)(2,1)S(1)} %copy-done.31), channel_id=1, source_target_pairs={{0,15},{1,14},{2,13},{3,12},{4,11},{5,10},{6,9},{7,8},{8,7},{9,6},... | collective-permute-start | bytes 786440 | tf_op jit(solution)/shard_map/ppermute | solution.py:399
  178.0 97.5 %copy-start = (bf16[8,128,128]{2,1,0:T(8,128)(2,1)}, bf16[8,128,128]{2,1,0:T(8,128)(2,1)S(1)}, u32[]{:S(2)}) copy-start(bf16[8,128,128]{2,1,0:T(8,128)(2,1)S(1)} %collective-permute-done.13.refs_1_) | copy-start | bytes 786436
  178.0 32.4 %collective-permute-start.18 = (bf16[8,128,128]{2,1,0:T(8,128)(2,1)}, bf16[8,128,128]{2,1,0:T(8,128)(2,1)S(1)}, u32[]{:S(2)}, u32[]{:S(2)}) collective-permute-start(bf16[8,128,128]{2,1,0:T(8,128)(2,1)} %get-tuple-element.64), channel_id=1, source_target_pairs={{0,20},{1,21},{2,22},{3,23},{4,16},{5,17},{6,18},{7,19},{8,28},{9,... | collective-permute-start | bytes 786440 | tf_op jit(solution)/shard_map/ppermute | solution.py:399
  186.5 24.6 %collective-permute-start.19 = (bf16[8,128,128]{2,1,0:T(8,128)(2,1)}, bf16[8,128,128]{2,1,0:T(8,128)(2,1)S(1)}, u32[]{:S(2)}, u32[]{:S(2)}) collective-permute-start(bf16[8,128,128]{2,1,0:T(8,128)(2,1)} %get-tuple-element.65), channel_id=1, source_target_pairs={{0,16},{1,17},{2,18},{3,19},{4,20},{5,21},{6,22},{7,23},{8,24},{9,... | collective-permute-start | bytes 786440 | tf_op jit(solution)/shard_map/ppermute | solution.py:399
  201.1 19.4 %collective-permute-start.23 = (bf16[8,128,128]{2,1,0:T(8,128)(2,1)}, bf16[8,128,128]{2,1,0:T(8,128)(2,1)S(1)}, u32[]{:S(2)}, u32[]{:S(2)}) collective-permute-start(bf16[8,128,128]{2,1,0:T(8,128)(2,1)} %get-tuple-element.68), channel_id=1, source_target_pairs={{0,18},{1,19},{2,16},{3,17},{4,22},{5,23},{6,20},{7,21},{8,26},{9,... | collective-permute-start | bytes 786440 | tf_op jit(solution)/shard_map/ppermute | solution.py:399
  201.8 25.2 %collective-permute-start.24 = (bf16[8,128,128]{2,1,0:T(8,128)(2,1)}, bf16[8,128,128]{2,1,0:T(8,128)(2,1)S(1)}, u32[]{:S(2)}, u32[]{:S(2)}) collective-permute-start(bf16[8,128,128]{2,1,0:T(8,128)(2,1)} %get-tuple-element.69), channel_id=1, source_target_pairs={{0,22},{1,23},{2,20},{3,21},{4,18},{5,19},{6,16},{7,17},{8,30},{9,... | collective-permute-start | bytes 786440 | tf_op jit(solution)/shard_map/ppermute | solution.py:399
  204.8 28.4 %collective-permute-start.25 = (bf16[8,128,128]{2,1,0:T(8,128)(2,1)}, bf16[8,128,128]{2,1,0:T(8,128)(2,1)S(1)}, u32[]{:S(2)}, u32[]{:S(2)}) collective-permute-start(bf16[8,128,128]{2,1,0:T(8,128)(2,1)} %get-tuple-element.70), channel_id=1, source_target_pairs={{0,21},{1,20},{2,23},{3,22},{4,17},{5,16},{6,19},{7,18},{8,29},{9,... | collective-permute-start | bytes 786440 | tf_op jit(solution)/shard_map/ppermute | solution.py:399
  211.1 22.1 %collective-permute-start.26 = (bf16[8,128,128]{2,1,0:T(8,128)(2,1)}, bf16[8,128,128]{2,1,0:T(8,128)(2,1)S(1)}, u32[]{:S(2)}, u32[]{:S(2)}) collective-permute-start(bf16[8,128,128]{2,1,0:T(8,128)(2,1)} %get-tuple-element.71), channel_id=1, source_target_pairs={{0,9},{1,8},{2,11},{3,10},{4,13},{5,12},{6,15},{7,14},{8,1},{9,0},... | collective-permute-start | bytes 786440 | tf_op jit(solution)/shard_map/ppermute | solution.py:399
  211.9 31.4 %collective-permute-start.27 = (bf16[8,128,128]{2,1,0:T(8,128)(2,1)}, bf16[8,128,128]{2,1,0:T(8,128)(2,1)S(1)}, u32[]{:S(2)}, u32[]{:S(2)}) collective-permute-start(bf16[8,128,128]{2,1,0:T(8,128)(2,1)} %get-tuple-element.72), channel_id=1, source_target_pairs={{0,11},{1,10},{2,9},{3,8},{4,15},{5,14},{6,13},{7,12},{8,3},{9,2},... | collective-permute-start | bytes 786440 | tf_op jit(solution)/shard_map/ppermute | solution.py:399
  220.5 25.6 %collective-permute-start.28 = (bf16[8,128,128]{2,1,0:T(8,128)(2,1)}, bf16[8,128,128]{2,1,0:T(8,128)(2,1)S(1)}, u32[]{:S(2)}, u32[]{:S(2)}) collective-permute-start(bf16[8,128,128]{2,1,0:T(8,128)(2,1)} %get-tuple-element.73), channel_id=1, source_target_pairs={{0,23},{1,22},{2,21},{3,20},{4,19},{5,18},{6,17},{7,16},{8,31},{9,... | collective-permute-start | bytes 786440 | tf_op jit(solution)/shard_map/ppermute | solution.py:399
  227.0 38.8 %collective-permute-start.29 = (bf16[8,128,128]{2,1,0:T(8,128)(2,1)}, bf16[8,128,128]{2,1,0:T(8,128)(2,1)S(1)}, u32[]{:S(2)}, u32[]{:S(2)}) collective-permute-start(bf16[8,128,128]{2,1,0:T(8,128)(2,1)} %get-tuple-element.74), channel_id=1, source_target_pairs={{0,28},{1,29},{2,30},{3,31},{4,24},{5,25},{6,26},{7,27},{8,20},{9,... | collective-permute-start | bytes 786440 | tf_op jit(solution)/shard_map/ppermute | solution.py:399
  233.2 33.4 %collective-permute-start.30 = (bf16[8,128,128]{2,1,0:T(8,128)(2,1)}, bf16[8,128,128]{2,1,0:T(8,128)(2,1)S(1)}, u32[]{:S(2)}, u32[]{:S(2)}) collective-permute-start(bf16[8,128,128]{2,1,0:T(8,128)(2,1)} %get-tuple-element.75), channel_id=1, source_target_pairs={{0,8},{1,9},{2,10},{3,11},{4,12},{5,13},{6,14},{7,15},{8,0},{9,1},... | collective-permute-start | bytes 786440 | tf_op jit(solution)/shard_map/ppermute | solution.py:399
  233.9 35.2 %collective-permute-start.31 = (bf16[8,128,128]{2,1,0:T(8,128)(2,1)}, bf16[8,128,128]{2,1,0:T(8,128)(2,1)S(1)}, u32[]{:S(2)}, u32[]{:S(2)}) collective-permute-start(bf16[8,128,128]{2,1,0:T(8,128)(2,1)} %get-tuple-element.76), channel_id=1, source_target_pairs={{0,10},{1,11},{2,8},{3,9},{4,14},{5,15},{6,12},{7,13},{8,2},{9,3},... | collective-permute-start | bytes 786440 | tf_op jit(solution)/shard_map/ppermute | solution.py:399
  243.9 28.7 %collective-permute-start.32 = (bf16[8,128,128]{2,1,0:T(8,128)(2,1)}, bf16[8,128,128]{2,1,0:T(8,128)(2,1)S(1)}, u32[]{:S(2)}, u32[]{:S(2)}) collective-permute-start(bf16[8,128,128]{2,1,0:T(8,128)(2,1)} %get-tuple-element.77), channel_id=1, source_target_pairs={{0,30},{1,31},{2,28},{3,29},{4,26},{5,27},{6,24},{7,25},{8,22},{9,... | collective-permute-start | bytes 786440 | tf_op jit(solution)/shard_map/ppermute | solution.py:399
  246.8 35.8 %collective-permute-start.33 = (bf16[8,128,128]{2,1,0:T(8,128)(2,1)}, bf16[8,128,128]{2,1,0:T(8,128)(2,1)}, u32[]{:S(2)}, u32[]{:S(2)}) collective-permute-start(bf16[8,128,128]{2,1,0:T(8,128)(2,1)} %get-tuple-element.78), channel_id=1, source_target_pairs={{0,29},{1,28},{2,31},{3,30},{4,25},{5,24},{6,27},{7,26},{8,21},{9,... | collective-permute-start | bytes 786440 | tf_op jit(solution)/shard_map/ppermute | solution.py:399
  266.5 26.0 %collective-permute-start.34 = (bf16[8,128,128]{2,1,0:T(8,128)(2,1)}, bf16[8,128,128]{2,1,0:T(8,128)(2,1)}, u32[]{:S(2)}, u32[]{:S(2)}) collective-permute-start(bf16[8,128,128]{2,1,0:T(8,128)(2,1)} %get-tuple-element.79), channel_id=1, source_target_pairs={{0,1},{1,0},{2,3},{3,2},{4,5},{5,4},{6,7},{7,6},{8,9},{9,8},{10,11... | collective-permute-start | bytes 786440 | tf_op jit(solution)/shard_map/ppermute | solution.py:399
  267.3 28.4 %collective-permute-start.35 = (bf16[8,128,128]{2,1,0:T(8,128)(2,1)}, bf16[8,128,128]{2,1,0:T(8,128)(2,1)}, u32[]{:S(2)}, u32[]{:S(2)}) collective-permute-start(bf16[8,128,128]{2,1,0:T(8,128)(2,1)} %get-tuple-element.80), channel_id=1, source_target_pairs={{0,3},{1,2},{2,1},{3,0},{4,7},{5,6},{6,5},{7,4},{8,11},{9,10},{10,... | collective-permute-start | bytes 786440 | tf_op jit(solution)/shard_map/ppermute | solution.py:399
  269.9 25.8 %collective-permute-start.36 = (bf16[8,128,128]{2,1,0:T(8,128)(2,1)}, bf16[8,128,128]{2,1,0:T(8,128)(2,1)}, u32[]{:S(2)}, u32[]{:S(2)}) collective-permute-start(bf16[8,128,128]{2,1,0:T(8,128)(2,1)} %get-tuple-element.81), channel_id=1, source_target_pairs={{0,31},{1,30},{2,29},{3,28},{4,27},{5,26},{6,25},{7,24},{8,23},{9,... | collective-permute-start | bytes 786440 | tf_op jit(solution)/shard_map/ppermute | solution.py:399
  273.3 24.3 %collective-permute-start.37 = (bf16[8,128,128]{2,1,0:T(8,128)(2,1)}, bf16[8,128,128]{2,1,0:T(8,128)(2,1)}, u32[]{:S(2)}, u32[]{:S(2)}) collective-permute-start(bf16[8,128,128]{2,1,0:T(8,128)(2,1)} %get-tuple-element.82), channel_id=1, source_target_pairs={{0,2},{1,3},{2,0},{3,1},{4,6},{5,7},{6,4},{7,5},{8,10},{9,11},{10,... | collective-permute-start | bytes 786440 | tf_op jit(solution)/shard_map/ppermute | solution.py:399
  282.6 15.3 %collective-permute-start.44 = (f32[8,128]{1,0:T(8,128)}, f32[8,128]{1,0:T(8,128)S(1)}, u32[]{:S(2)}, u32[]{:S(2)}) collective-permute-start(f32[8,128]{1,0:T(8,128)} %get-tuple-element.83.refs_1_), channel_id=1, source_target_pairs={{0,7},{1,6},{2,5},{3,4},{4,3},{5,2},{6,1},{7,0},{8,15},{9,14},{10,... | collective-permute-start | bytes 12296 | tf_op jit(solution)/shard_map/ppermute | solution.py:355
  292.5 9.0 %collective-permute-start.43 = (f32[8,128]{1,0:T(8,128)}, f32[8,128]{1,0:T(8,128)S(1)}, u32[]{:S(2)}, u32[]{:S(2)}) collective-permute-start(f32[8,128]{1,0:T(8,128)} %get-tuple-element.83.refs_1_), channel_id=1, source_target_pairs={{0,6},{1,7},{2,4},{3,5},{4,2},{5,3},{6,0},{7,1},{8,14},{9,15},{10,... | collective-permute-start | bytes 12296 | tf_op jit(solution)/shard_map/ppermute | solution.py:355
  295.6 13.4 %collective-permute-start.42 = (f32[8,128]{1,0:T(8,128)}, f32[8,128]{1,0:T(8,128)S(1)}, u32[]{:S(2)}, u32[]{:S(2)}) collective-permute-start(f32[8,128]{1,0:T(8,128)} %get-tuple-element.83.refs_1_), channel_id=1, source_target_pairs={{0,5},{1,4},{2,7},{3,6},{4,1},{5,0},{6,3},{7,2},{8,13},{9,12},{10,... | collective-permute-start | bytes 12296 | tf_op jit(solution)/shard_map/ppermute | solution.py:355
  295.6 13.4 %collective-permute-start.41 = (f32[8,128]{1,0:T(8,128)}, f32[8,128]{1,0:T(8,128)S(1)}, u32[]{:S(2)}, u32[]{:S(2)}) collective-permute-start(f32[8,128]{1,0:T(8,128)} %get-tuple-element.83.refs_1_), channel_id=1, source_target_pairs={{0,4},{1,5},{2,6},{3,7},{4,0},{5,1},{6,2},{7,3},{8,12},{9,13},{10,... | collective-permute-start | bytes 12296 | tf_op jit(solution)/shard_map/ppermute | solution.py:355
  297.7 11.4 %collective-permute-start.40 = (f32[8,128]{1,0:T(8,128)}, f32[8,128]{1,0:T(8,128)S(1)}, u32[]{:S(2)}, u32[]{:S(2)}) collective-permute-start(f32[8,128]{1,0:T(8,128)} %get-tuple-element.83.refs_1_), channel_id=1, source_target_pairs={{0,3},{1,2},{2,1},{3,0},{4,7},{5,6},{6,5},{7,4},{8,11},{9,10},{10,... | collective-permute-start | bytes 12296 | tf_op jit(solution)/shard_map/ppermute | solution.py:355
  297.9 11.2 %collective-permute-start.39 = (f32[8,128]{1,0:T(8,128)}, f32[8,128]{1,0:T(8,128)S(1)}, u32[]{:S(2)}, u32[]{:S(2)}) collective-permute-start(f32[8,128]{1,0:T(8,128)} %get-tuple-element.83.refs_1_), channel_id=1, source_target_pairs={{0,2},{1,3},{2,0},{3,1},{4,6},{5,7},{6,4},{7,5},{8,10},{9,11},{10,... | collective-permute-start | bytes 12296 | tf_op jit(solution)/shard_map/ppermute | solution.py:355
  301.5 7.6 %collective-permute-start.38 = (f32[8,128]{1,0:T(8,128)}, f32[8,128]{1,0:T(8,128)S(1)}, u32[]{:S(2)}, u32[]{:S(2)}) collective-permute-start(f32[8,128]{1,0:T(8,128)} %get-tuple-element.83.refs_1_), channel_id=1, source_target_pairs={{0,1},{1,0},{2,3},{3,2},{4,5},{5,4},{6,7},{7,6},{8,9},{9,8},{10,11... | collective-permute-start | bytes 12296 | tf_op jit(solution)/shard_map/ppermute | solution.py:355
  (35 other events, 268.6 us)

commit v2 on v1

--- a/solution.py
+++ b/solution.py
@@ -135,9 +135,14 @@
     return lax.shift_right_logical(index, size.bit_length() - 1), index & (size - 1)
 
 
-def project_kernel(meta_ref, dens, top, bottom, left, right, wcol, wrow, acc_in, *refs,
+def project_kernel(meta_ref, dens, top, bottom, left, right, wcol, wrow, *refs,
                    layout, first, count, block_rows, block_cols, has_local):
     capacity = layout.capacity
+    if first:
+        acc = refs[0][...]
+        refs = refs[1:]
+    else:
+        acc = jnp.zeros((8, BS), jnp.float32)
     outs, acc_out = refs[:count], refs[count]
     buf, fetch_sem, lines, tiles, store_sem = refs[count + 1:]
     pairs = count * capacity // 2
@@ -253,7 +258,7 @@
         along_columns(pair)
         return acc
 
-    acc = lax.fori_loop(1, pairs, body, acc_in[...])
+    acc = lax.fori_loop(1, pairs, body, acc)
     acc_out[...] = along_rows(pairs - 1, acc)
 
     stores = []
@@ -289,7 +294,8 @@
     results = pl.pallas_call(
         kernel,
         out_shape=tuple(shapes) + (jax.ShapeDtypeStruct((8, BS), jnp.float32),),
-        in_specs=[pl.BlockSpec(memory_space=pltpu.SMEM)] + [anywhere] * 5 + [vmem] * 3,
+        in_specs=[pl.BlockSpec(memory_space=pltpu.SMEM)] + [anywhere] * 5
+        + [vmem] * (2 + len(acc)),
         out_specs=tuple([anywhere] * count + [vmem]),
         scratch_shapes=[
             pltpu.VMEM((BUFFERS, 2, PAD, WIDE), jnp.float32),
@@ -301,7 +307,7 @@
         cost_estimate=pl.CostEstimate(
             flops=steps * 300_000_000, bytes_accessed=steps * 300_000, transcendentals=0),
         name="project",
-    )(meta, *fields, acc)
+    )(meta, *fields, *acc)
     return results[:-1], results[-1]
 
 
@@ -387,11 +393,11 @@
 
     unit = max(1, 8 // capacity)
     groups = grouped(order, [unit * size for size in GROUPS])
-    acc = jnp.zeros((8, BS), jnp.float32)
+    acc = None
     arrivals, first = [], 0
     for group in groups:
         sent, acc = project(
-            meta, fields, acc, layout=layout, first=first, count=len(group),
+            meta, fields, () if acc is None else (acc,), layout=layout, first=first, count=len(group),
             block_rows=block_rows, block_cols=block_cols, has_local=group[-1] == 0)
         for offset, part in zip(group, sent):
             if offset:

time: 313 us -> 313 us (level)
  no operation moved by 1% of the time
where the time goes in v2:
time: 313 us; the launch traced here: 311 us
  Pallas kernels  99.8 us (32%)
  waiting for transfers between devices  94.6 us (30%)
  starting transfers between devices  94 us (30%)
  local copies, waits for them, and re-layouts  17.7 us (6%)
  other arithmetic  3.15 us (1%)
    ppermute x31, waiting for transfers between devices, per_device(): part = lax.ppermute(part, AXES, pairs)  92.7 us
    pallas_call x6, Pallas kernels, project(): pl.pallas_call(kernel, out_shape=tuple(shapes) + (jax.ShapeDtypeStruct((8...  82.6 us
    ppermute x31, starting transfers between devices, per_device(): part = lax.ppermute(part, AXES, pairs)  68.9 us
    pallas_call x9, Pallas kernels, place(): pl.pallas_call(functools.partial(place_kernel, layout=layout, first=first...  17.2 us
    ppermute x10, starting transfers between devices, spread(): part = lax.ppermute(value, axis, [(i, i ^ offset) for i in range(count)])  13.9 us
    unnamed x79, local copies, waits for them, and re-layouts  10.6 us
  transfers between devices with their start and end apart: 45, of which 13 were waited for; matrix products, arithmetic and copies ran while one was open for 3% of the time, Pallas kernels for 30%

profile of v2, /device:TPU:0, one launch (start us, length us, event | category | flops | bytes accessed | tf_op | source)
XLA Modules:
  0.0 310.8 jit_solution(8310452552555434337)
XLA Ops:
  3.0 3.0 collective-permute-start
  14.9 5.5 %collective-permute-start.2 = (f32[16,1056]{1,0:T(8,128)S(1)}, f32[16,1056]{1,0:T(8,128)S(1)}, u32[]{:S(2)}, u32[]{:S(2)}) collective-permute-start(f32[16,1056]{1,0:T(8,128)S(1)} %concatenate.18), channel_id=1, source_target_pairs={{0,1},{1,2},{2,3},{3,4},{4,5},{5,6},{6,7},{8,9},{9,10},{10,11},{11... | collective-permute-start | bytes 202760 | tf_op jit(solution)/shard_map/ppermute | solution.py:92
  24.5 5.3 %project.6 = (bf16[8,128,128]{2,1,0:T(8,128)(2,1)}, f32[8,128]{1,0:T(8,128)}) custom-call(s32[768]{0:T(1024)} %copy-done.30, f32[1024,4096]{1,0:T(8,128)} %dens.11, f32[16,4096]{1,0:T(8,128)} %copy-done.29, f32[16,4096]{1,0:T(8,128)} %copy-done.28, f32[1056,128]{1,0:T(8,128)} %pad_bitcast_fusion.1.left, f32[1056,128]{1,0:T(8,128)} %pad_bitcast_fusion.right, ...), custom_call_target="tpu_custom_call" | custom-call | flops 2400000000 | bytes 2400000 | tf_op jit(solution)/shard_map/project/pallas_call | solution.py:294
  29.8 5.7 %collective-permute-start.4 = (bf16[8,128,128]{2,1,0:T(8,128)(2,1)}, bf16[8,128,128]{2,1,0:T(8,128)(2,1)S(1)}, u32[]{:S(2)}, u32[]{:S(2)}) collective-permute-start(bf16[8,128,128]{2,1,0:T(8,128)(2,1)} %get-tuple-element.50), channel_id=1, source_target_pairs={{0,4},{1,5},{2,6},{3,7},{4,0},{5,1},{6,2},{7,3},{8,12},{9,13},{10,... | collective-permute-start | bytes 786440 | tf_op jit(solution)/shard_map/ppermute | solution.py:405
  35.5 7.3 %project.7 = (bf16[8,128,128]{2,1,0:T(8,128)(2,1)}, bf16[8,128,128]{2,1,0:T(8,128)(2,1)}, f32[8,128]{1,0:T(8,128)}) custom-call(s32[768]{0:T(1024)} %copy-done.30, f32[1024,4096]{1,0:T(8,128)} %dens.11, f32[16,4096]{1,0:T(8,128)} %copy-done.29, f32[16,4096]{1,0:T(8,128)} %copy-done.28, f32[1056,128]{1,0:T(8,128)} %pad_bitcast_fusion.1.left, ...), custom_call_target="tpu_custom_call" | custom-call | flops 4800000000 | bytes 4800000 | tf_op jit(solution)/shard_map/project/pallas_call | solution.py:294
  42.7 11.2 %project.8 = (bf16[8,128,128]{2,1,0:T(8,128)(2,1)}, bf16[8,128,128]{2,1,0:T(8,128)(2,1)}, bf16[8,128,128]{2,1,0:T(8,128)(2,1)}, bf16[8,128,128]{2,1,0:T(8,128)(2,1)}, f32[8,128]{1,0:T(8,128)}) custom-call(s32[768]{0:T(1024)} %copy-done.30, f32[1024,4096]{1,0:T(8,128)} %dens.11, f32[16,4096]{1,0:T(8,128)} %copy-done.29, f32[16,4096]{1,0:T(8,128)} %copy-done.28, ...), custom_call_target="tpu_custom_call" | custom-call | flops 9600000000 | bytes 9600000 | tf_op jit(solution)/shard_map/project/pallas_call | solution.py:294
  53.9 18.9 %project.9 = (bf16[8,128,128]{2,1,0:T(8,128)(2,1)}, bf16[8,128,128]{2,1,0:T(8,128)(2,1)}, bf16[8,128,128]{2,1,0:T(8,128)(2,1)}, bf16[8,128,128]{2,1,0:T(8,128)(2...) custom-call(s32[768]{0:T(1024)} %copy-done.30, ...), custom_call_target="tpu_custom_call" | custom-call | flops 19200000000 | bytes 19200000 | tf_op jit(solution)/shard_map/project/pallas_call | solution.py:294
  72.9 18.9 %project.10 = (bf16[8,128,128]{2,1,0:T(8,128)(2,1)}, bf16[8,128,128]{2,1,0:T(8,128)(2,1)}, bf16[8,128,128]{2,1,0:T(8,128)(2,1)}, bf16[8,128,128]{2,1,0:T(8,128)(...) custom-call(s32[768]{0:T(1024)} %copy-done.30, ...), custom_call_target="tpu_custom_call" | custom-call | flops 19200000000 | bytes 19200000 | tf_op jit(solution)/shard_map/project/pallas_call | solution.py:294
  91.9 20.9 %project.11 = (bf16[8,128,128]{2,1,0:T(8,128)(2,1)}, bf16[8,128,128]{2,1,0:T(8,128)(2,1)}, bf16[8,128,128]{2,1,0:T(8,128)(2,1)}, bf16[8,128,128]{2,1,0:T(8,128)(...) custom-call(s32[768]{0:T(1024)} %copy-done.30, ...), custom_call_target="tpu_custom_call" | custom-call | flops 21600000000 | bytes 21600000 | tf_op jit(solution)/shard_map/project/pallas_call | solution.py:294
  116.9 1.6 collective-permute-start.7
  118.6 1.8 collective-permute-start.8
  120.4 3.1 collective-permute-start.9
  123.5 2.3 collective-permute-done.5.refs_1_
  125.8 8.6 %collective-permute-start.10 = (bf16[8,128,128]{2,1,0:T(8,128)(2,1)}, bf16[8,128,128]{2,1,0:T(8,128)(2,1)S(1)}, u32[]{:S(2)}, u32[]{:S(2)}) collective-permute-start(bf16[8,128,128]{2,1,0:T(8,128)(2,1)} %get-tuple-element.56), channel_id=1, source_target_pairs={{0,12},{1,13},{2,14},{3,15},{4,8},{5,9},{6,10},{7,11},{8,4},{9,5},... | collective-permute-start | bytes 786440 | tf_op jit(solution)/shard_map/ppermute | solution.py:405
  134.4 17.7 %collective-permute-done.6.refs_2_ = bf16[8,128,128]{2,1,0:T(8,128)(2,1)S(1)} collective-permute-done((bf16[8,128,128]{2,1,0:T(8,128)(2,1)S(1)}, bf16[8,128,128]{2,1,0:T(8,128)(2,1)S(1)}, u32[]{:S(2)}, u32[]{:S(2)}) %collective-permute-start.6) | collective-permute-done | bytes 262176 | tf_op jit(solution)/shard_map/ppermute | solution.py:405
  152.2 1.6 collective-permute-start.13
  153.9 4.4 %collective-permute-start.14 = (bf16[8,128,128]{2,1,0:T(8,128)(2,1)}, bf16[8,128,128]{2,1,0:T(8,128)(2,1)S(1)}, u32[]{:S(2)}, u32[]{:S(2)}) collective-permute-start(bf16[8,128,128]{2,1,0:T(8,128)(2,1)} %get-tuple-element.60), channel_id=1, source_target_pairs={{0,13},{1,12},{2,15},{3,14},{4,9},{5,8},{6,11},{7,10},{8,5},{9,4},... | collective-permute-start | bytes 786440 | tf_op jit(solution)/shard_map/ppermute | solution.py:405
  158.2 15.3 %collective-permute-done.10.refs_2_ = bf16[8,128,128]{2,1,0:T(8,128)(2,1)S(1)} collective-permute-done((bf16[8,128,128]{2,1,0:T(8,128)(2,1)}, bf16[8,128,128]{2,1,0:T(8,128)(2,1)S(1)}, u32[]{:S(2)}, u32[]{:S(2)}) %collective-permute-start.10) | collective-permute-done | bytes 262176 | tf_op jit(solution)/shard_map/ppermute | solution.py:405
  173.6 2.4 collective-permute-start.16
  177.4 3.3 %collective-permute-start.18 = (bf16[8,128,128]{2,1,0:T(8,128)(2,1)}, bf16[8,128,128]{2,1,0:T(8,128)(2,1)S(1)}, u32[]{:S(2)}, u32[]{:S(2)}) collective-permute-start(bf16[8,128,128]{2,1,0:T(8,128)(2,1)} %get-tuple-element.64), channel_id=1, source_target_pairs={{0,20},{1,21},{2,22},{3,23},{4,16},{5,17},{6,18},{7,19},{8,28},{9,... | collective-permute-start | bytes 786440 | tf_op jit(solution)/shard_map/ppermute | solution.py:405
  180.7 4.3 %collective-permute-done.14.refs_2_ = bf16[8,128,128]{2,1,0:T(8,128)(2,1)S(1)} collective-permute-done((bf16[8,128,128]{2,1,0:T(8,128)(2,1)}, bf16[8,128,128]{2,1,0:T(8,128)(2,1)S(1)}, u32[]{:S(2)}, u32[]{:S(2)}) %collective-permute-start.14) | collective-permute-done | bytes 262176 | tf_op jit(solution)/shard_map/ppermute | solution.py:405
  186.0 13.8 %collective-permute-done.15.refs_3_ = bf16[8,128,128]{2,1,0:T(8,128)(2,1)S(1)} collective-permute-done((bf16[8,128,128]{2,1,0:T(8,128)(2,1)S(1)}, bf16[8,128,128]{2,1,0:T(8,128)(2,1)S(1)}, u32[]{:S(2)}, u32[]{:S(2)}) %collective-permute-start.15) | collective-permute-done | bytes 262176 | tf_op jit(solution)/shard_map/ppermute | solution.py:405
  201.2 2.2 collective-permute-start.24
  204.2 1.5 collective-permute-start.25
  205.7 4.0 %collective-permute-done.18.refs_2_ = bf16[8,128,128]{2,1,0:T(8,128)(2,1)S(1)} collective-permute-done((bf16[8,128,128]{2,1,0:T(8,128)(2,1)}, bf16[8,128,128]{2,1,0:T(8,128)(2,1)S(1)}, u32[]{:S(2)}, u32[]{:S(2)}) %collective-permute-start.18) | collective-permute-done | bytes 262176 | tf_op jit(solution)/shard_map/ppermute | solution.py:405
  211.1 8.7 %collective-permute-done.23.refs_0_ = bf16[8,128,128]{2,1,0:T(8,128)(2,1)S(1)} collective-permute-done((bf16[8,128,128]{2,1,0:T(8,128)(2,1)}, bf16[8,128,128]{2,1,0:T(8,128)(2,1)S(1)}, u32[]{:S(2)}, u32[]{:S(2)}) %collective-permute-start.23) | collective-permute-done | bytes 262176 | tf_op jit(solution)/shard_map/ppermute | solution.py:405
  219.8 6.6 %collective-permute-start.28 = (bf16[8,128,128]{2,1,0:T(8,128)(2,1)}, bf16[8,128,128]{2,1,0:T(8,128)(2,1)S(1)}, u32[]{:S(2)}, u32[]{:S(2)}) collective-permute-start(bf16[8,128,128]{2,1,0:T(8,128)(2,1)} %get-tuple-element.73), channel_id=1, source_target_pairs={{0,23},{1,22},{2,21},{3,20},{4,19},{5,18},{6,17},{7,16},{8,31},{9,... | collective-permute-start | bytes 786440 | tf_op jit(solution)/shard_map/ppermute | solution.py:405
  226.8 5.8 %collective-permute-done.25.refs_2_ = bf16[8,128,128]{2,1,0:T(8,128)(2,1)S(1)} collective-permute-done((bf16[8,128,128]{2,1,0:T(8,128)(2,1)}, bf16[8,128,128]{2,1,0:T(8,128)(2,1)S(1)}, u32[]{:S(2)}, u32[]{:S(2)}) %collective-permute-start.25) | collective-permute-done | bytes 262176 | tf_op jit(solution)/shard_map/ppermute | solution.py:405
  233.3 9.3 %collective-permute-start.31 = (bf16[8,128,128]{2,1,0:T(8,128)(2,1)}, bf16[8,128,128]{2,1,0:T(8,128)(2,1)S(1)}, u32[]{:S(2)}, u32[]{:S(2)}) collective-permute-start(bf16[8,128,128]{2,1,0:T(8,128)(2,1)} %get-tuple-element.76), channel_id=1, source_target_pairs={{0,10},{1,11},{2,8},{3,9},{4,14},{5,15},{6,12},{7,13},{8,2},{9,3},... | collective-permute-start | bytes 786440 | tf_op jit(solution)/shard_map/ppermute | solution.py:405
  243.3 2.1 collective-permute-start.32
  246.1 5.3 %collective-permute-start.33 = (bf16[8,128,128]{2,1,0:T(8,128)(2,1)}, bf16[8,128,128]{2,1,0:T(8,128)(2,1)}, u32[]{:S(2)}, u32[]{:S(2)}) collective-permute-start(bf16[8,128,128]{2,1,0:T(8,128)(2,1)} %get-tuple-element.78), channel_id=1, source_target_pairs={{0,29},{1,28},{2,31},{3,30},{4,25},{5,24},{6,27},{7,26},{8,21},{9,... | collective-permute-start | bytes 786440 | tf_op jit(solution)/shard_map/ppermute | solution.py:405
  251.4 13.8 %collective-permute-done.29.refs_2_ = bf16[8,128,128]{2,1,0:T(8,128)(2,1)S(1)} collective-permute-done((bf16[8,128,128]{2,1,0:T(8,128)(2,1)}, bf16[8,128,128]{2,1,0:T(8,128)(2,1)S(1)}, u32[]{:S(2)}, u32[]{:S(2)}) %collective-permute-start.29) | collective-permute-done | bytes 262176 | tf_op jit(solution)/shard_map/ppermute | solution.py:405
  266.7 1.8 collective-permute-start.35
  269.3 2.8 collective-permute-start.36
  273.3 1.7 place.9.out_in
  275.0 1.8 place.10.out_in
  277.8 1.8 place.11.out_in
  279.6 2.4 place.12
  282.0 3.2 %collective-permute-start.44 = (f32[8,128]{1,0:T(8,128)}, f32[8,128]{1,0:T(8,128)S(1)}, u32[]{:S(2)}, u32[]{:S(2)}) collective-permute-start(f32[8,128]{1,0:T(8,128)} %get-tuple-element.83.refs_1_), channel_id=1, source_target_pairs={{0,7},{1,6},{2,5},{3,4},{4,3},{5,2},{6,1},{7,0},{8,15},{9,14},{10,... | collective-permute-start | bytes 12296 | tf_op jit(solution)/shard_map/ppermute | solution.py:361
  285.2 6.8 %collective-permute-done.34.refs_3_ = bf16[8,128,128]{2,1,0:T(8,128)(2,1)} collective-permute-done((bf16[8,128,128]{2,1,0:T(8,128)(2,1)}, bf16[8,128,128]{2,1,0:T(8,128)(2,1)}, u32[]{:S(2)}, u32[]{:S(2)}) %collective-permute-start.34) | collective-permute-done | bytes 262176 | tf_op jit(solution)/shard_map/ppermute | solution.py:405
  292.0 3.0 collective-permute-start.43
  295.0 2.0 collective-permute-start.41
  297.4 3.4 %collective-permute-start.39 = (f32[8,128]{1,0:T(8,128)}, f32[8,128]{1,0:T(8,128)S(1)}, u32[]{:S(2)}, u32[]{:S(2)}) collective-permute-start(f32[8,128]{1,0:T(8,128)} %get-tuple-element.83.refs_1_), channel_id=1, source_target_pairs={{0,2},{1,3},{2,0},{3,1},{4,6},{5,7},{6,4},{7,5},{8,10},{9,11},{10,... | collective-permute-start | bytes 12296 | tf_op jit(solution)/shard_map/ppermute | solution.py:361
  300.9 1.8 place.13.out_in
  302.7 1.8 place.14.out_in
  304.5 2.0 place.15.out_in
  306.5 1.8 place.16.out_in
  308.4 2.2 place.17
  (167 shorter events, 32.6 us)
Async XLA Ops:
  1.7 11.2 %collective-permute-start.1 = (f32[16,4096]{1,0:T(8,128)S(1)}, f32[16,4096]{1,0:T(8,128)S(1)}, u32[]{:S(2)}, u32[]{:S(2)}) collective-permute-start(f32[16,4096]{1,0:T(8,128)S(1)} %get-tuple-element.90), channel_id=1, source_target_pairs={{8,0},{16,8},{24,16},{9,1},{17,9},{25,17},{10,2},{18,10},{26,18},{... | collective-permute-start | bytes 786440 | tf_op jit(solution)/shard_map/ppermute | solution.py:85
  3.0 10.1 %collective-permute-start = (f32[16,4096]{1,0:T(8,128)S(1)}, f32[16,4096]{1,0:T(8,128)S(1)}, u32[]{:S(2)}, u32[]{:S(2)}) collective-permute-start(f32[16,4096]{1,0:T(8,128)S(1)} %get-tuple-element.91), channel_id=1, source_target_pairs={{0,8},{8,16},{16,24},{1,9},{9,17},{17,25},{2,10},{10,18},{18,26},{... | collective-permute-start | bytes 786440 | tf_op jit(solution)/shard_map/ppermute | solution.py:84
  13.3 7.3 %collective-permute-start.3 = (f32[16,1056]{1,0:T(8,128)S(1)}, f32[16,1056]{1,0:T(8,128)S(1)}, u32[]{:S(2)}, u32[]{:S(2)}) collective-permute-start(f32[16,1056]{1,0:T(8,128)S(1)} %concatenate.19), channel_id=1, source_target_pairs={{1,0},{2,1},{3,2},{4,3},{5,4},{6,5},{7,6},{9,8},{10,9},{11,10},{12... | collective-permute-start | bytes 202760 | tf_op jit(solution)/shard_map/ppermute | solution.py:93
  14.9 8.3 %collective-permute-start.2 = (f32[16,1056]{1,0:T(8,128)S(1)}, f32[16,1056]{1,0:T(8,128)S(1)}, u32[]{:S(2)}, u32[]{:S(2)}) collective-permute-start(f32[16,1056]{1,0:T(8,128)S(1)} %concatenate.18), channel_id=1, source_target_pairs={{0,1},{1,2},{2,3},{3,4},{4,5},{5,6},{6,7},{8,9},{9,10},{10,11},{11... | collective-permute-start | bytes 202760 | tf_op jit(solution)/shard_map/ppermute | solution.py:92
  29.8 90.6 %collective-permute-start.4 = (bf16[8,128,128]{2,1,0:T(8,128)(2,1)}, bf16[8,128,128]{2,1,0:T(8,128)(2,1)S(1)}, u32[]{:S(2)}, u32[]{:S(2)}) collective-permute-start(bf16[8,128,128]{2,1,0:T(8,128)(2,1)} %get-tuple-element.50), channel_id=1, source_target_pairs={{0,4},{1,5},{2,6},{3,7},{4,0},{5,1},{6,2},{7,3},{8,12},{9,13},{10,... | collective-permute-start | bytes 786440 | tf_op jit(solution)/shard_map/ppermute | solution.py:405
  91.9 81.7 %copy-start.32 = (bf16[8,128,128]{2,1,0:T(8,128)(2,1)S(1)}, bf16[8,128,128]{2,1,0:T(8,128)(2,1)}, u32[]{:S(2)}) copy-start(bf16[8,128,128]{2,1,0:T(8,128)(2,1)} %get-tuple-element.62) | copy-start | bytes 786436
  91.9 84.2 %copy-start.31 = (bf16[8,128,128]{2,1,0:T(8,128)(2,1)S(1)}, bf16[8,128,128]{2,1,0:T(8,128)(2,1)}, u32[]{:S(2)}) copy-start(bf16[8,128,128]{2,1,0:T(8,128)(2,1)} %get-tuple-element.63) | copy-start | bytes 786436
  112.8 3.3 %collective-permute-start.22 = (f32[8,128]{1,0:T(8,128)}, f32[8,128]{1,0:T(8,128)S(1)}, u32[]{:S(2)}, u32[]{:S(2)}) collective-permute-start(f32[8,128]{1,0:T(8,128)} %get-tuple-element.66.refs_4_), channel_id=1, source_target_pairs={{0,24},{8,16},{16,8},{24,0},{1,25},{9,17},{17,9},{25,1},{2,26},{10... | collective-permute-start | bytes 12296 | tf_op jit(solution)/shard_map/ppermute | solution.py:361
  112.9 4.1 %collective-permute-start.21 = (f32[8,128]{1,0:T(8,128)}, f32[8,128]{1,0:T(8,128)S(1)}, u32[]{:S(2)}, u32[]{:S(2)}) collective-permute-start(f32[8,128]{1,0:T(8,128)} %get-tuple-element.66.refs_4_), channel_id=1, source_target_pairs={{0,16},{8,24},{16,0},{24,8},{1,17},{9,25},{17,1},{25,9},{2,18},{10... | collective-permute-start | bytes 12296 | tf_op jit(solution)/shard_map/ppermute | solution.py:361
  114.2 4.4 %collective-permute-start.20 = (f32[8,128]{1,0:T(8,128)}, f32[8,128]{1,0:T(8,128)S(1)}, u32[]{:S(2)}, u32[]{:S(2)}) collective-permute-start(f32[8,128]{1,0:T(8,128)} %get-tuple-element.66.refs_4_), channel_id=1, source_target_pairs={{0,8},{8,0},{16,24},{24,16},{1,9},{9,1},{17,25},{25,17},{2,10},{10... | collective-permute-start | bytes 12296 | tf_op jit(solution)/shard_map/ppermute | solution.py:361
  114.7 11.1 %collective-permute-start.5 = (bf16[8,128,128]{2,1,0:T(8,128)(2,1)S(1)}, bf16[8,128,128]{2,1,0:T(8,128)(2,1)S(1)}, u32[]{:S(2)}, u32[]{:S(2)}) collective-permute-start(bf16[8,128,128]{2,1,0:T(8,128)(2,1)S(1)} %copy-done.37), channel_id=1, source_target_pairs={{0,6},{1,7},{2,4},{3,5},{4,2},{5,3},{6,0},{7,1},{8,14},{9,15},{10,... | collective-permute-start | bytes 786440 | tf_op jit(solution)/shard_map/ppermute | solution.py:405
  116.1 36.0 %collective-permute-start.6 = (bf16[8,128,128]{2,1,0:T(8,128)(2,1)S(1)}, bf16[8,128,128]{2,1,0:T(8,128)(2,1)S(1)}, u32[]{:S(2)}, u32[]{:S(2)}) collective-permute-start(bf16[8,128,128]{2,1,0:T(8,128)(2,1)S(1)} %copy-done.36), channel_id=1, source_target_pairs={{0,5},{1,4},{2,7},{3,6},{4,1},{5,0},{6,3},{7,2},{8,13},{9,12},{10,... | collective-permute-start | bytes 786440 | tf_op jit(solution)/shard_map/ppermute | solution.py:405
  116.9 35.2 %collective-permute-start.7 = (bf16[8,128,128]{2,1,0:T(8,128)(2,1)S(1)}, bf16[8,128,128]{2,1,0:T(8,128)(2,1)S(1)}, u32[]{:S(2)}, u32[]{:S(2)}) collective-permute-start(bf16[8,128,128]{2,1,0:T(8,128)(2,1)S(1)} %copy-done.35), channel_id=1, source_target_pairs={{0,25},{1,24},{2,27},{3,26},{4,29},{5,28},{6,31},{7,30},{8,17},{9,... | collective-permute-start | bytes 786440 | tf_op jit(solution)/shard_map/ppermute | solution.py:405
  118.6 33.7 %collective-permute-start.8 = (bf16[8,128,128]{2,1,0:T(8,128)(2,1)S(1)}, bf16[8,128,128]{2,1,0:T(8,128)(2,1)S(1)}, u32[]{:S(2)}, u32[]{:S(2)}) collective-permute-start(bf16[8,128,128]{2,1,0:T(8,128)(2,1)S(1)} %copy-done.34), channel_id=1, source_target_pairs={{0,27},{1,26},{2,25},{3,24},{4,31},{5,30},{6,29},{7,28},{8,19},{9,... | collective-permute-start | bytes 786440 | tf_op jit(solution)/shard_map/ppermute | solution.py:405
  120.4 33.5 %collective-permute-start.9 = (bf16[8,128,128]{2,1,0:T(8,128)(2,1)}, bf16[8,128,128]{2,1,0:T(8,128)(2,1)S(1)}, u32[]{:S(2)}, u32[]{:S(2)}) collective-permute-start(bf16[8,128,128]{2,1,0:T(8,128)(2,1)} %get-tuple-element.55), channel_id=1, source_target_pairs={{0,7},{1,6},{2,5},{3,4},{4,3},{5,2},{6,1},{7,0},{8,15},{9,14},{10,... | collective-permute-start | bytes 786440 | tf_op jit(solution)/shard_map/ppermute | solution.py:405
  125.8 47.7 %collective-permute-start.10 = (bf16[8,128,128]{2,1,0:T(8,128)(2,1)}, bf16[8,128,128]{2,1,0:T(8,128)(2,1)S(1)}, u32[]{:S(2)}, u32[]{:S(2)}) collective-permute-start(bf16[8,128,128]{2,1,0:T(8,128)(2,1)} %get-tuple-element.56), channel_id=1, source_target_pairs={{0,12},{1,13},{2,14},{3,15},{4,8},{5,9},{6,10},{7,11},{8,4},{9,5},... | collective-permute-start | bytes 786440 | tf_op jit(solution)/shard_map/ppermute | solution.py:405
  152.1 21.5 %collective-permute-start.11 = (bf16[8,128,128]{2,1,0:T(8,128)(2,1)}, bf16[8,128,128]{2,1,0:T(8,128)(2,1)S(1)}, u32[]{:S(2)}, u32[]{:S(2)}) collective-permute-start(bf16[8,128,128]{2,1,0:T(8,128)(2,1)} %get-tuple-element.57), channel_id=1, source_target_pairs={{0,24},{1,25},{2,26},{3,27},{4,28},{5,29},{6,30},{7,31},{8,16},{9,... | collective-permute-start | bytes 786440 | tf_op jit(solution)/shard_map/ppermute | solution.py:405
  152.1 23.9 %collective-permute-start.12 = (bf16[8,128,128]{2,1,0:T(8,128)(2,1)}, bf16[8,128,128]{2,1,0:T(8,128)(2,1)S(1)}, u32[]{:S(2)}, u32[]{:S(2)}) collective-permute-start(bf16[8,128,128]{2,1,0:T(8,128)(2,1)} %get-tuple-element.58), channel_id=1, source_target_pairs={{0,26},{1,27},{2,24},{3,25},{4,30},{5,31},{6,28},{7,29},{8,18},{9,... | collective-permute-start | bytes 786440 | tf_op jit(solution)/shard_map/ppermute | solution.py:405
  152.2 25.2 %collective-permute-start.13 = (bf16[8,128,128]{2,1,0:T(8,128)(2,1)}, bf16[8,128,128]{2,1,0:T(8,128)(2,1)S(1)}, u32[]{:S(2)}, u32[]{:S(2)}) collective-permute-start(bf16[8,128,128]{2,1,0:T(8,128)(2,1)} %get-tuple-element.59), channel_id=1, source_target_pairs={{0,14},{1,15},{2,12},{3,13},{4,10},{5,11},{6,8},{7,9},{8,6},{9,7},... | collective-permute-start | bytes 786440 | tf_op jit(solution)/shard_map/ppermute | solution.py:405
  153.9 31.2 %collective-permute-start.14 = (bf16[8,128,128]{2,1,0:T(8,128)(2,1)}, bf16[8,128,128]{2,1,0:T(8,128)(2,1)S(1)}, u32[]{:S(2)}, u32[]{:S(2)}) collective-permute-start(bf16[8,128,128]{2,1,0:T(8,128)(2,1)} %get-tuple-element.60), channel_id=1, source_target_pairs={{0,13},{1,12},{2,15},{3,14},{4,9},{5,8},{6,11},{7,10},{8,5},{9,4},... | collective-permute-start | bytes 786440 | tf_op jit(solution)/shard_map/ppermute | solution.py:405
  173.6 26.3 %collective-permute-start.15 = (bf16[8,128,128]{2,1,0:T(8,128)(2,1)S(1)}, bf16[8,128,128]{2,1,0:T(8,128)(2,1)S(1)}, u32[]{:S(2)}, u32[]{:S(2)}) collective-permute-start(bf16[8,128,128]{2,1,0:T(8,128)(2,1)S(1)} %copy-done.33), channel_id=1, source_target_pairs={{0,17},{1,16},{2,19},{3,18},{4,21},{5,20},{6,23},{7,22},{8,25},{9,... | collective-permute-start | bytes 786440 | tf_op jit(solution)/shard_map/ppermute | solution.py:405
  173.6 26.9 %collective-permute-start.16 = (bf16[8,128,128]{2,1,0:T(8,128)(2,1)S(1)}, bf16[8,128,128]{2,1,0:T(8,128)(2,1)S(1)}, u32[]{:S(2)}, u32[]{:S(2)}) collective-permute-start(bf16[8,128,128]{2,1,0:T(8,128)(2,1)S(1)} %copy-done.32), channel_id=1, source_target_pairs={{0,19},{1,18},{2,17},{3,16},{4,23},{5,22},{6,21},{7,20},{8,27},{9,... | collective-permute-start | bytes 786440 | tf_op jit(solution)/shard_map/ppermute | solution.py:405
  176.0 27.4 %collective-permute-start.17 = (bf16[8,128,128]{2,1,0:T(8,128)(2,1)S(1)}, bf16[8,128,128]{2,1,0:T(8,128)(2,1)S(1)}, u32[]{:S(2)}, u32[]{:S(2)}) collective-permute-start(bf16[8,128,128]{2,1,0:T(8,128)(2,1)S(1)} %copy-done.31), channel_id=1, source_target_pairs={{0,15},{1,14},{2,13},{3,12},{4,11},{5,10},{6,9},{7,8},{8,7},{9,6},... | collective-permute-start | bytes 786440 | tf_op jit(solution)/shard_map/ppermute | solution.py:405
  177.4 97.6 %copy-start = (bf16[8,128,128]{2,1,0:T(8,128)(2,1)}, bf16[8,128,128]{2,1,0:T(8,128)(2,1)S(1)}, u32[]{:S(2)}) copy-start(bf16[8,128,128]{2,1,0:T(8,128)(2,1)S(1)} %collective-permute-done.13.refs_1_) | copy-start | bytes 786436
  177.4 32.3 %collective-permute-start.18 = (bf16[8,128,128]{2,1,0:T(8,128)(2,1)}, bf16[8,128,128]{2,1,0:T(8,128)(2,1)S(1)}, u32[]{:S(2)}, u32[]{:S(2)}) collective-permute-start(bf16[8,128,128]{2,1,0:T(8,128)(2,1)} %get-tuple-element.64), channel_id=1, source_target_pairs={{0,20},{1,21},{2,22},{3,23},{4,16},{5,17},{6,18},{7,19},{8,28},{9,... | collective-permute-start | bytes 786440 | tf_op jit(solution)/shard_map/ppermute | solution.py:405
  185.8 24.6 %collective-permute-start.19 = (bf16[8,128,128]{2,1,0:T(8,128)(2,1)}, bf16[8,128,128]{2,1,0:T(8,128)(2,1)S(1)}, u32[]{:S(2)}, u32[]{:S(2)}) collective-permute-start(bf16[8,128,128]{2,1,0:T(8,128)(2,1)} %get-tuple-element.65), channel_id=1, source_target_pairs={{0,16},{1,17},{2,18},{3,19},{4,20},{5,21},{6,22},{7,23},{8,24},{9,... | collective-permute-start | bytes 786440 | tf_op jit(solution)/shard_map/ppermute | solution.py:405
  200.5 19.3 %collective-permute-start.23 = (bf16[8,128,128]{2,1,0:T(8,128)(2,1)}, bf16[8,128,128]{2,1,0:T(8,128)(2,1)S(1)}, u32[]{:S(2)}, u32[]{:S(2)}) collective-permute-start(bf16[8,128,128]{2,1,0:T(8,128)(2,1)} %get-tuple-element.68), channel_id=1, source_target_pairs={{0,18},{1,19},{2,16},{3,17},{4,22},{5,23},{6,20},{7,21},{8,26},{9,... | collective-permute-start | bytes 786440 | tf_op jit(solution)/shard_map/ppermute | solution.py:405
  201.2 25.2 %collective-permute-start.24 = (bf16[8,128,128]{2,1,0:T(8,128)(2,1)}, bf16[8,128,128]{2,1,0:T(8,128)(2,1)S(1)}, u32[]{:S(2)}, u32[]{:S(2)}) collective-permute-start(bf16[8,128,128]{2,1,0:T(8,128)(2,1)} %get-tuple-element.69), channel_id=1, source_target_pairs={{0,22},{1,23},{2,20},{3,21},{4,18},{5,19},{6,16},{7,17},{8,30},{9,... | collective-permute-start | bytes 786440 | tf_op jit(solution)/shard_map/ppermute | solution.py:405
  204.2 28.4 %collective-permute-start.25 = (bf16[8,128,128]{2,1,0:T(8,128)(2,1)}, bf16[8,128,128]{2,1,0:T(8,128)(2,1)S(1)}, u32[]{:S(2)}, u32[]{:S(2)}) collective-permute-start(bf16[8,128,128]{2,1,0:T(8,128)(2,1)} %get-tuple-element.70), channel_id=1, source_target_pairs={{0,21},{1,20},{2,23},{3,22},{4,17},{5,16},{6,19},{7,18},{8,29},{9,... | collective-permute-start | bytes 786440 | tf_op jit(solution)/shard_map/ppermute | solution.py:405
  210.4 22.2 %collective-permute-start.26 = (bf16[8,128,128]{2,1,0:T(8,128)(2,1)}, bf16[8,128,128]{2,1,0:T(8,128)(2,1)S(1)}, u32[]{:S(2)}, u32[]{:S(2)}) collective-permute-start(bf16[8,128,128]{2,1,0:T(8,128)(2,1)} %get-tuple-element.71), channel_id=1, source_target_pairs={{0,9},{1,8},{2,11},{3,10},{4,13},{5,12},{6,15},{7,14},{8,1},{9,0},... | collective-permute-start | bytes 786440 | tf_op jit(solution)/shard_map/ppermute | solution.py:405
  211.1 31.5 %collective-permute-start.27 = (bf16[8,128,128]{2,1,0:T(8,128)(2,1)}, bf16[8,128,128]{2,1,0:T(8,128)(2,1)S(1)}, u32[]{:S(2)}, u32[]{:S(2)}) collective-permute-start(bf16[8,128,128]{2,1,0:T(8,128)(2,1)} %get-tuple-element.72), channel_id=1, source_target_pairs={{0,11},{1,10},{2,9},{3,8},{4,15},{5,14},{6,13},{7,12},{8,3},{9,2},... | collective-permute-start | bytes 786440 | tf_op jit(solution)/shard_map/ppermute | solution.py:405
  219.8 25.6 %collective-permute-start.28 = (bf16[8,128,128]{2,1,0:T(8,128)(2,1)}, bf16[8,128,128]{2,1,0:T(8,128)(2,1)S(1)}, u32[]{:S(2)}, u32[]{:S(2)}) collective-permute-start(bf16[8,128,128]{2,1,0:T(8,128)(2,1)} %get-tuple-element.73), channel_id=1, source_target_pairs={{0,23},{1,22},{2,21},{3,20},{4,19},{5,18},{6,17},{7,16},{8,31},{9,... | collective-permute-start | bytes 786440 | tf_op jit(solution)/shard_map/ppermute | solution.py:405
  226.4 38.9 %collective-permute-start.29 = (bf16[8,128,128]{2,1,0:T(8,128)(2,1)}, bf16[8,128,128]{2,1,0:T(8,128)(2,1)S(1)}, u32[]{:S(2)}, u32[]{:S(2)}) collective-permute-start(bf16[8,128,128]{2,1,0:T(8,128)(2,1)} %get-tuple-element.74), channel_id=1, source_target_pairs={{0,28},{1,29},{2,30},{3,31},{4,24},{5,25},{6,26},{7,27},{8,20},{9,... | collective-permute-start | bytes 786440 | tf_op jit(solution)/shard_map/ppermute | solution.py:405
  232.6 33.4 %collective-permute-start.30 = (bf16[8,128,128]{2,1,0:T(8,128)(2,1)}, bf16[8,128,128]{2,1,0:T(8,128)(2,1)S(1)}, u32[]{:S(2)}, u32[]{:S(2)}) collective-permute-start(bf16[8,128,128]{2,1,0:T(8,128)(2,1)} %get-tuple-element.75), channel_id=1, source_target_pairs={{0,8},{1,9},{2,10},{3,11},{4,12},{5,13},{6,14},{7,15},{8,0},{9,1},... | collective-permute-start | bytes 786440 | tf_op jit(solution)/shard_map/ppermute | solution.py:405
  233.3 35.3 %collective-permute-start.31 = (bf16[8,128,128]{2,1,0:T(8,128)(2,1)}, bf16[8,128,128]{2,1,0:T(8,128)(2,1)S(1)}, u32[]{:S(2)}, u32[]{:S(2)}) collective-permute-start(bf16[8,128,128]{2,1,0:T(8,128)(2,1)} %get-tuple-element.76), channel_id=1, source_target_pairs={{0,10},{1,11},{2,8},{3,9},{4,14},{5,15},{6,12},{7,13},{8,2},{9,3},... | collective-permute-start | bytes 786440 | tf_op jit(solution)/shard_map/ppermute | solution.py:405
  243.3 28.8 %collective-permute-start.32 = (bf16[8,128,128]{2,1,0:T(8,128)(2,1)}, bf16[8,128,128]{2,1,0:T(8,128)(2,1)S(1)}, u32[]{:S(2)}, u32[]{:S(2)}) collective-permute-start(bf16[8,128,128]{2,1,0:T(8,128)(2,1)} %get-tuple-element.77), channel_id=1, source_target_pairs={{0,30},{1,31},{2,28},{3,29},{4,26},{5,27},{6,24},{7,25},{8,22},{9,... | collective-permute-start | bytes 786440 | tf_op jit(solution)/shard_map/ppermute | solution.py:405
  246.1 35.9 %collective-permute-start.33 = (bf16[8,128,128]{2,1,0:T(8,128)(2,1)}, bf16[8,128,128]{2,1,0:T(8,128)(2,1)}, u32[]{:S(2)}, u32[]{:S(2)}) collective-permute-start(bf16[8,128,128]{2,1,0:T(8,128)(2,1)} %get-tuple-element.78), channel_id=1, source_target_pairs={{0,29},{1,28},{2,31},{3,30},{4,25},{5,24},{6,27},{7,26},{8,21},{9,... | collective-permute-start | bytes 786440 | tf_op jit(solution)/shard_map/ppermute | solution.py:405
  266.0 26.0 %collective-permute-start.34 = (bf16[8,128,128]{2,1,0:T(8,128)(2,1)}, bf16[8,128,128]{2,1,0:T(8,128)(2,1)}, u32[]{:S(2)}, u32[]{:S(2)}) collective-permute-start(bf16[8,128,128]{2,1,0:T(8,128)(2,1)} %get-tuple-element.79), channel_id=1, source_target_pairs={{0,1},{1,0},{2,3},{3,2},{4,5},{5,4},{6,7},{7,6},{8,9},{9,8},{10,11... | collective-permute-start | bytes 786440 | tf_op jit(solution)/shard_map/ppermute | solution.py:405
  266.7 28.2 %collective-permute-start.35 = (bf16[8,128,128]{2,1,0:T(8,128)(2,1)}, bf16[8,128,128]{2,1,0:T(8,128)(2,1)}, u32[]{:S(2)}, u32[]{:S(2)}) collective-permute-start(bf16[8,128,128]{2,1,0:T(8,128)(2,1)} %get-tuple-element.80), channel_id=1, source_target_pairs={{0,3},{1,2},{2,1},{3,0},{4,7},{5,6},{6,5},{7,4},{8,11},{9,10},{10,... | collective-permute-start | bytes 786440 | tf_op jit(solution)/shard_map/ppermute | solution.py:405
  269.3 25.7 %collective-permute-start.36 = (bf16[8,128,128]{2,1,0:T(8,128)(2,1)}, bf16[8,128,128]{2,1,0:T(8,128)(2,1)}, u32[]{:S(2)}, u32[]{:S(2)}) collective-permute-start(bf16[8,128,128]{2,1,0:T(8,128)(2,1)} %get-tuple-element.81), channel_id=1, source_target_pairs={{0,31},{1,30},{2,29},{3,28},{4,27},{5,26},{6,25},{7,24},{8,23},{9,... | collective-permute-start | bytes 786440 | tf_op jit(solution)/shard_map/ppermute | solution.py:405
  272.8 24.2 %collective-permute-start.37 = (bf16[8,128,128]{2,1,0:T(8,128)(2,1)}, bf16[8,128,128]{2,1,0:T(8,128)(2,1)}, u32[]{:S(2)}, u32[]{:S(2)}) collective-permute-start(bf16[8,128,128]{2,1,0:T(8,128)(2,1)} %get-tuple-element.82), channel_id=1, source_target_pairs={{0,2},{1,3},{2,0},{3,1},{4,6},{5,7},{6,4},{7,5},{8,10},{9,11},{10,... | collective-permute-start | bytes 786440 | tf_op jit(solution)/shard_map/ppermute | solution.py:405
  282.0 15.3 %collective-permute-start.44 = (f32[8,128]{1,0:T(8,128)}, f32[8,128]{1,0:T(8,128)S(1)}, u32[]{:S(2)}, u32[]{:S(2)}) collective-permute-start(f32[8,128]{1,0:T(8,128)} %get-tuple-element.83.refs_1_), channel_id=1, source_target_pairs={{0,7},{1,6},{2,5},{3,4},{4,3},{5,2},{6,1},{7,0},{8,15},{9,14},{10,... | collective-permute-start | bytes 12296 | tf_op jit(solution)/shard_map/ppermute | solution.py:361
  292.0 8.8 %collective-permute-start.43 = (f32[8,128]{1,0:T(8,128)}, f32[8,128]{1,0:T(8,128)S(1)}, u32[]{:S(2)}, u32[]{:S(2)}) collective-permute-start(f32[8,128]{1,0:T(8,128)} %get-tuple-element.83.refs_1_), channel_id=1, source_target_pairs={{0,6},{1,7},{2,4},{3,5},{4,2},{5,3},{6,0},{7,1},{8,14},{9,15},{10,... | collective-permute-start | bytes 12296 | tf_op jit(solution)/shard_map/ppermute | solution.py:361
  294.9 13.4 %collective-permute-start.42 = (f32[8,128]{1,0:T(8,128)}, f32[8,128]{1,0:T(8,128)S(1)}, u32[]{:S(2)}, u32[]{:S(2)}) collective-permute-start(f32[8,128]{1,0:T(8,128)} %get-tuple-element.83.refs_1_), channel_id=1, source_target_pairs={{0,5},{1,4},{2,7},{3,6},{4,1},{5,0},{6,3},{7,2},{8,13},{9,12},{10,... | collective-permute-start | bytes 12296 | tf_op jit(solution)/shard_map/ppermute | solution.py:361
  295.0 13.4 %collective-permute-start.41 = (f32[8,128]{1,0:T(8,128)}, f32[8,128]{1,0:T(8,128)S(1)}, u32[]{:S(2)}, u32[]{:S(2)}) collective-permute-start(f32[8,128]{1,0:T(8,128)} %get-tuple-element.83.refs_1_), channel_id=1, source_target_pairs={{0,4},{1,5},{2,6},{3,7},{4,0},{5,1},{6,2},{7,3},{8,12},{9,13},{10,... | collective-permute-start | bytes 12296 | tf_op jit(solution)/shard_map/ppermute | solution.py:361
  297.0 11.4 %collective-permute-start.40 = (f32[8,128]{1,0:T(8,128)}, f32[8,128]{1,0:T(8,128)S(1)}, u32[]{:S(2)}, u32[]{:S(2)}) collective-permute-start(f32[8,128]{1,0:T(8,128)} %get-tuple-element.83.refs_1_), channel_id=1, source_target_pairs={{0,3},{1,2},{2,1},{3,0},{4,7},{5,6},{6,5},{7,4},{8,11},{9,10},{10,... | collective-permute-start | bytes 12296 | tf_op jit(solution)/shard_map/ppermute | solution.py:361
  297.4 11.1 %collective-permute-start.39 = (f32[8,128]{1,0:T(8,128)}, f32[8,128]{1,0:T(8,128)S(1)}, u32[]{:S(2)}, u32[]{:S(2)}) collective-permute-start(f32[8,128]{1,0:T(8,128)} %get-tuple-element.83.refs_1_), channel_id=1, source_target_pairs={{0,2},{1,3},{2,0},{3,1},{4,6},{5,7},{6,4},{7,5},{8,10},{9,11},{10,... | collective-permute-start | bytes 12296 | tf_op jit(solution)/shard_map/ppermute | solution.py:361
  300.8 7.6 %collective-permute-start.38 = (f32[8,128]{1,0:T(8,128)}, f32[8,128]{1,0:T(8,128)S(1)}, u32[]{:S(2)}, u32[]{:S(2)}) collective-permute-start(f32[8,128]{1,0:T(8,128)} %get-tuple-element.83.refs_1_), channel_id=1, source_target_pairs={{0,1},{1,0},{2,3},{3,2},{4,5},{5,4},{6,7},{7,6},{8,9},{9,8},{10,11... | collective-permute-start | bytes 12296 | tf_op jit(solution)/shard_map/ppermute | solution.py:361
  (35 other events, 266.8 us)
